TPU v7x, 256 devices: a whole 4x4x8 slice. The times are simulated.
256 devices in a mesh: seq: 64 (over x_hi, z, y), kvh: 4 (over x_lo, core).
Axes of the slice: x: 4 (x_hi: 2, x_lo: 2; x = x_hi * 2 + x_lo), y: 4, z: 8, core: 2. Of those that a mesh axis runs over, the one named last changes fastest.
Arguments:
- queries: bfloat16 [8192, 8192], P('seq', 'kvh'), may hold values from -100 to 100
- keys: bfloat16 [8192, 1024], P('seq', 'kvh'), may hold values from -4 to 4
- values: bfloat16 [8192, 1024], P('seq', 'kvh'), may hold values from -6 to 6
- segments: int32 [8192], P('seq'), may hold values from 0 to 2, never falling along the last dimension, each value on 1 to 4224 neighbouring positions
- basis: bfloat16 [8, 2, 128, 32], P('kvh'), may hold values from -0.5 to 0.5
Outputs:
- attention: bfloat16 [8192, 8192], P('seq', 'kvh')
- latents: bfloat16 [8192, 512], P('seq', 'kvh')
- captured: float32 [8, 2, 32, 32], P('kvh')
- share: float32 [8, 2], P('kvh')
Inputs may be any that keep to these rules, and one draw needn't show every extreme that they name: `segments`: document ids never fall along the sequence, and each document has at most 4224 tokens.
All inputs are finite; a program needn't handle non-finite values.
Results may differ from a plain program's by a relative error of at most 0.004.
Values may be sent and summed in bfloat16 or wider, within the bound.
No kernel may reach another device: no remote copies, remote signals or barrier semaphores. Data moves between devices by JAX's collectives and lax.ppermute only.
A program may use at most 64 MiB of HBM per device.

v0:
```python
import functools
import math

import jax
import jax.numpy as jnp
from jax import lax
from jax.experimental import pallas as pl
from jax.experimental.pallas import tpu as pltpu
from jax.sharding import Mesh
from jax.sharding import PartitionSpec as P

HD = 128
KVH = 8
RANK = 32
TOKENS = 8192
SLABS = 16
SEQ = ("a", "z", "y")
KV = ("xl", "c")
RING = ("a", "z")
COLUMN = ("y", "c")
BLOCK = 144
HALF = 2 * BLOCK
RIDER = 32
SCALE2 = HD**-0.5 * math.log2(math.e)
FIRST = -1e30
MASKED = -2e30
FAR = 1e9


def to_heads(t):
    pairs = []
    for y in range(4):
        for c in range(2):
            head = (y & 1) ^ t
            pairs.append((y * 2 + c, (2 * c + head) * 2 + (y >> 1)))
    return pairs


def shifted(array, by):
    return lax.ppermute(array, RING, [(i, (i + by) % SLABS) for i in range(SLABS)])


def added(array, axis, distance):
    size = lax.axis_size(axis)
    return array + lax.ppermute(array, axis, [(i, i ^ distance) for i in range(size)])


def place():
    slab = lax.axis_index("a") * 8 + lax.axis_index("z")
    return slab, lax.axis_index("c"), lax.axis_index("y") & 1


def encoded(total):
    high = total.astype(jnp.bfloat16)
    rest = (total - high.astype(jnp.float32)).astype(jnp.bfloat16)
    return high, rest


def put(ref, row, total):
    ref[row : row + RIDER, 0:128], ref[row : row + RIDER, 128:256] = encoded(total)


def got(ref, row):
    rows = slice(row, row + RIDER)
    return ref[rows, 0:128].astype(jnp.float32) + ref[rows, 128:256].astype(jnp.float32)


def put_wide(ref, total):
    for n, part in enumerate(encoded(total)):
        for m in range(2):
            lanes = slice(m * 256 + n * 128, m * 256 + n * 128 + 128)
            ref[128:BLOCK, lanes] = part[m * 16 : (m + 1) * 16, :]


def got_wide(ref):
    rows = []
    for m in range(2):
        high = ref[128:BLOCK, m * 256 : m * 256 + 128].astype(jnp.float32)
        rest = ref[128:BLOCK, m * 256 + 128 : m * 256 + 256].astype(jnp.float32)
        rows.append(high + rest)
    return jnp.concatenate(rows, axis=0)


def prepare_kernel(
    keys_hbm,
    values_hbm,
    segments_hbm,
    basis_hbm,
    first_ref,
    second_ref,
    latents_ref,
    energy_ref,
    keys_ref,
    values_ref,
    segments_ref,
    basis_ref,
    semaphores,
):
    loads = [
        pltpu.make_async_copy(source, target, semaphores.at[n])
        for n, (source, target) in enumerate(
            (
                (segments_hbm, segments_ref),
                (keys_hbm, keys_ref),
                (values_hbm, values_ref),
                (basis_hbm, basis_ref),
            )
        )
    ]
    for copy in loads:
        copy.start()
    for copy in loads:
        copy.wait()
    ids = segments_ref[...]
    n1 = jnp.sum((ids < 1).astype(jnp.float32))
    n2 = jnp.sum((ids < 2).astype(jnp.float32))
    lanes = lax.broadcasted_iota(jnp.int32, (16, 256), 1)
    counts = jnp.where(lanes < 128, n1, n2).astype(jnp.bfloat16)
    projected, energies = [], []
    for g in range(2):
        for kind, ref in enumerate((keys_ref, values_ref)):
            rows = ref[:, g * HD : (g + 1) * HD]
            projected.append(
                lax.dot_general(
                    rows,
                    basis_ref[g, kind],
                    (((1,), (1,)), ((), ())),
                    preferred_element_type=jnp.float32,
                )
            )
            squares = rows.astype(jnp.float32)
            energies.append(jnp.sum(squares * squares))
    latents = jnp.concatenate(projected, axis=1)
    latents_ref[...] = latents.astype(jnp.bfloat16)
    seen = lax.dot_general(
        latents,
        latents,
        (((0,), (0,)), ((), ())),
        precision=lax.Precision.HIGHEST,
        preferred_element_type=jnp.float32,
    )
    lane = lax.broadcasted_iota(jnp.int32, (RIDER, 128), 1) // RANK
    row = lax.broadcasted_iota(jnp.int32, (RIDER, 128), 0)
    riders = []
    for g in range(2):
        other = jnp.where(row == 0, energies[2 * g], jnp.where(row == 1, energies[2 * g + 1], 0.0))
        for n in (2 * g, 2 * g + 1):
            other = jnp.where(lane == n, seen[n * RANK : (n + 1) * RANK, :], other)
        riders.append(other)
    row8 = lax.broadcasted_iota(jnp.int32, (8, 128), 0)
    energy_ref[...] = jnp.where(
        row8 == 0,
        energies[0] + energies[2],
        jnp.where(row8 == 1, energies[1] + energies[3], 0.0),
    )
    for odd in range(2):

        @pl.when(place()[2] == odd)
        def _(odd=odd):
            for ref, head in ((first_ref, odd), (second_ref, 1 - odd)):
                ref[0:128, 0:HD] = keys_ref[:, head * HD : (head + 1) * HD]
                ref[0:128, HD : 2 * HD] = values_ref[:, head * HD : (head + 1) * HD]
                put(ref, BLOCK, riders[head])

    for ref in (first_ref, second_ref):
        ref[128:BLOCK, :] = counts


def start_kernel(first_ref, second_ref, energy_ref, out_ref):
    out_ref[0:BLOCK, :] = first_ref[0:BLOCK, :]
    out_ref[BLOCK:HALF, :] = second_ref[0:BLOCK, :]
    lane = lax.broadcasted_iota(jnp.int32, (RIDER, 128), 1) // 64
    row = lax.broadcasted_iota(jnp.int32, (RIDER, 128), 0)
    energy = jnp.where(
        row == 2, energy_ref[0:1, :], jnp.where(row == 3, energy_ref[1:2, :], 0.0)
    )
    energy = jnp.where(lane == 1 - place()[2], energy, 0.0)
    put(out_ref, HALF, got(first_ref, BLOCK) + got(second_ref, BLOCK) + energy)


def once_kernel(own_ref, eight_ref, up_ref, down_ref):
    both = got(own_ref, HALF) + got(eight_ref, HALF)
    up_ref[0:HALF, :] = own_ref[0:HALF, :]
    down_ref[0:HALF, :] = eight_ref[0:HALF, :]
    put(up_ref, HALF, both)
    put(down_ref, HALF, both)


def twice_kernel(up_ref, one_ref, down_ref, seven_ref, far_up_ref, far_down_ref):
    far_up_ref[0:HALF, :] = up_ref[0:HALF, :]
    far_up_ref[HALF : 2 * HALF, :] = one_ref[0:HALF, :]
    far_up_ref[2 * HALF : 2 * HALF + RIDER, :] = up_ref[HALF : HALF + RIDER, :]
    far_up_ref[2 * HALF + RIDER : 2 * HALF + 2 * RIDER, :] = one_ref[HALF : HALF + RIDER, :]
    far_down_ref[0:HALF, :] = down_ref[0:HALF, :]
    far_down_ref[HALF : 2 * HALF, :] = seven_ref[0:HALF, :]
    put(far_down_ref, 2 * HALF, got(down_ref, HALF) + got(seven_ref, HALF))


def tail_kernel(two_three_ref, eight_ref, out_ref):
    out_ref[0:HALF, :] = two_three_ref[HALF : 2 * HALF, :]
    for odd in range(2):

        @pl.when(place()[2] == odd)
        def _(odd=odd):
            row = (1 - odd) * BLOCK
            out_ref[HALF : HALF + BLOCK, :] = eight_ref[row : row + BLOCK, :]

    out_ref[HALF + BLOCK : HALF + BLOCK + RIDER, :] = two_three_ref[
        2 * HALF + RIDER : 2 * HALF + 2 * RIDER, :
    ]


def total_kernel(four_ref, up_ref, one_ref, seven_ref, two_three_ref, six_five_ref, out_ref, energy_ref):
    at = HALF + BLOCK
    out_ref[0:at, :] = four_ref[0:at, :]
    total = got(up_ref, HALF) + got(one_ref, HALF) + got(seven_ref, HALF)
    total += got(two_three_ref, 2 * HALF) + got(two_three_ref, 2 * HALF + RIDER)
    total += got(six_five_ref, 2 * HALF) + got(four_ref, at)
    put(out_ref, at, total)
    lane = lax.broadcasted_iota(jnp.int32, (RIDER, 128), 1) // 64
    row = lax.broadcasted_iota(jnp.int32, (RIDER, 128), 0)
    energies = (lane == 1 - place()[2]) & ((row == 2) | (row == 3))
    energy_ref[...] = jnp.where(energies, 2.0 * total, 0.0)


def attend_kernel(count, units, tiles, first, last, rider, *refs):
    refs = list(refs)
    if first:
        q_in = [refs.pop(0) for _ in range(2)]
    key_refs = [refs.pop(0) for _ in range(count)]
    state_in = None if first else [refs.pop(0) for _ in range(5)]
    if last:
        energy_ref = refs.pop(0)
        out_ref = refs.pop(0)
        q_ref = state_in[0]
        top_ref, sum_ref, mix_ref = refs
    else:
        q_ref, starts_ref, top_ref, sum_ref, mix_ref = refs
    slab, core, odd = place()
    origin = tiles[0] * 1024 if last else 0

    found_units = []
    for unit in units:
        found = []
        for array, row, distance, partner, rounds in unit:
            base = ((slab - distance) & (SLABS - 1)) * 512 + (1 - core if partner else core) * 256
            for n, t in enumerate(rounds):
                block = base + (128 if t is None else (odd ^ t) * 128)
                found.append((key_refs[array], row + n * BLOCK, block))
        found_units.append(found)

    one = jnp.full((16, 128), FAR, jnp.float32) if first else state_in[1][0:16, :]
    two = jnp.full((16, 128), FAR, jnp.float32) if first else state_in[1][16:32, :]
    for found in found_units:
        for ref, row, base in found:
            counts = ref[row + 128 : row + BLOCK, :].astype(jnp.float32)
            at = base.astype(jnp.float32)
            n1, n2 = counts[:, :128], counts[:, 128:]
            one = jnp.minimum(one, jnp.where(n1 < 128.0, at + n1, FAR))
            two = jnp.minimum(two, jnp.where(n2 < 128.0, at + n2, FAR))
    if not last:
        starts_ref[0:16, :] = one
        starts_ref[16:32, :] = two
    start1 = jnp.min(one).astype(jnp.int32)
    start2 = jnp.min(two).astype(jnp.int32)

    if first:
        for t in range(2):
            for j in range(8):
                q_ref[t * 1024 + j * 128 : t * 1024 + (j + 1) * 128, :] = q_in[t][
                    0:128, j * HD : (j + 1) * HD
                ]
        top_ref[...] = jnp.full(top_ref.shape, FIRST, jnp.float32)
        sum_ref[...] = jnp.zeros(sum_ref.shape, jnp.float32)
        mix_ref[...] = jnp.zeros(mix_ref.shape, jnp.float32)
    elif last:
        span = slice(origin, origin + 1024)
        top_ref[...] = state_in[2][span, :]
        sum_ref[...] = state_in[3][span, :]
        mix_ref[...] = state_in[4][span, :]

    row_iota = lax.broadcasted_iota(jnp.int32, (128, 128), 0)
    lane_iota = lax.broadcasted_iota(jnp.int32, (128, 128), 1)

    def low_of(position):
        return jnp.where(position >= start2, start2, jnp.where(position >= start1, start1, 0))

    q_base = {t: slab * 512 + core * 256 + (odd ^ t) * 128 for t in tiles}
    for found in found_units:
        needed = functools.reduce(
            jnp.logical_or,
            [
                (base <= q_base[t]) & (base + 127 >= low_of(q_base[t]))
                for t in tiles
                for ref, row, base in found
            ],
        )

        @pl.when(needed)
        def _(found=found):
            k = jnp.concatenate([r[row : row + 128, 0:HD] for r, row, _ in found], axis=0)
            v = jnp.concatenate([r[row : row + 128, HD : 2 * HD] for r, row, _ in found], axis=0)
            scores = {
                t: lax.dot_general(
                    q_ref[t * 1024 : (t + 1) * 1024, :],
                    k,
                    (((1,), (1,)), ((), ())),
                    preferred_element_type=jnp.float32,
                )
                for t in tiles
            }
            for t in tiles:
                q_pos = q_base[t] + row_iota
                lows = low_of(q_pos)
                parts = []
                for n, (ref, row, base) in enumerate(found):
                    k_pos = base + lane_iota
                    mask = (k_pos >= lows) & (k_pos <= q_pos)
                    mask = jnp.concatenate([mask] * 8, axis=0)
                    parts.append(
                        jnp.where(mask, scores[t][:, n * 128 : (n + 1) * 128], MASKED)
                    )
                best = functools.reduce(jnp.maximum, parts)
                span = slice(t * 1024 - origin, (t + 1) * 1024 - origin)
                top_old = top_ref[span, :]
                top = jnp.maximum(top_old, jnp.max(best, axis=1, keepdims=True))
                factor = jnp.exp2((top_old - top) * SCALE2)
                weights = [jnp.exp2((part - top) * SCALE2) for part in parts]
                sum_ref[span, :] = sum_ref[span, :] * factor + functools.reduce(jnp.add, weights)
                rounded = jnp.concatenate([w.astype(jnp.bfloat16) for w in weights], axis=1)
                mix_ref[span, :] = mix_ref[span, :] * factor + jnp.dot(
                    rounded, v, preferred_element_type=jnp.float32
                )
                top_ref[span, :] = top

    if last:
        for j in range(8):
            span = slice(j * 128, (j + 1) * 128)
            total = jnp.sum(sum_ref[span, :], axis=1, keepdims=True)
            out_ref[0:128, j * HD : (j + 1) * HD] = (mix_ref[span, :] / total).astype(jnp.bfloat16)
        total = got(key_refs[0], rider) + got(key_refs[1], rider) + energy_ref[...]
        put_wide(out_ref, total)
        out_ref[128:BLOCK, 512:1024] = jnp.zeros((16, 512), jnp.bfloat16)


def finish_kernel(first_ref, second_ref, attention_ref, captured_ref, share_ref):
    odd = place()[2]
    for swap in range(2):

        @pl.when(odd == swap)
        def _(swap=swap):
            for t, ref in enumerate((first_ref, second_ref)):
                head = t ^ swap
                attention_ref[:, head * 1024 : (head + 1) * 1024] = ref[0:128, :]

    received = [got_wide(first_ref), got_wide(second_ref)]
    row = lax.broadcasted_iota(jnp.int32, (RIDER, 128), 0)
    lane = lax.broadcasted_iota(jnp.int32, (RIDER, 128), 1)
    rows = lax.broadcasted_iota(jnp.int32, (2, 2), 0)
    columns = lax.broadcasted_iota(jnp.int32, (2, 2), 1)
    own, everything = {}, [0.0, 0.0]
    for g in range(2):
        sums = jnp.where(odd == g, received[0], received[1])
        for kind in range(2):
            n = 2 * g + kind
            captured_ref[n] = sums[:, n * RANK : (n + 1) * RANK] * (1.0 / TOKENS)
            here = lane == 64 * (1 - g)
            own[n] = jnp.sum(jnp.where(here & (row == kind), sums, 0.0))
            everything[kind] += 0.5 * jnp.sum(jnp.where(here & (row == kind + 2), sums, 0.0))
    share = jnp.zeros((2, 2), jnp.float32)
    for g in range(2):
        for kind in range(2):
            value = jnp.full((2, 2), KVH * own[2 * g + kind], jnp.float32) / everything[kind]
            share = jnp.where((rows == g) & (columns == kind), value, share)
    share_ref[...] = share


def vmem():
    return pl.BlockSpec(memory_space=pltpu.VMEM)


def rows(count):
    return jax.ShapeDtypeStruct((count, 256), jnp.bfloat16)


def small(kernel, out_shape, *inputs):
    return pl.pallas_call(
        kernel,
        out_shape=out_shape,
        in_specs=[vmem()] * len(inputs),
        out_specs=[vmem()] * len(out_shape),
        compiler_params=pltpu.CompilerParams(vmem_limit_bytes=6 * 1024 * 1024),
        cost_estimate=pl.CostEstimate(flops=1 << 20, bytes_accessed=1 << 18, transcendentals=0),
    )(*inputs)


def attend(q, arrays, units, state, tile=None, rider=None, energy=None):
    first, last = state is None, tile is not None
    wide = (2048, 128)
    carry = [
        jax.ShapeDtypeStruct(wide, jnp.bfloat16),
        jax.ShapeDtypeStruct((32, 128), jnp.float32),
        jax.ShapeDtypeStruct(wide, jnp.float32),
        jax.ShapeDtypeStruct(wide, jnp.float32),
        jax.ShapeDtypeStruct(wide, jnp.float32),
    ]
    tiles = (tile,) if last else (0, 1)
    keys = sum(128 * len(piece[4]) for unit in units for piece in unit)
    work = len(tiles) * 1024 * keys
    inputs = (list(q) if first else []) + list(arrays)
    aliases = {}
    if not first:
        if not last:
            aliases = {len(inputs) + n: n for n in range(5)}
        inputs += list(state)
    if last:
        inputs.append(energy)
        out_shape = [jax.ShapeDtypeStruct((BLOCK, 1024), jnp.bfloat16)]
        scratch = [pltpu.VMEM((1024, 128), jnp.float32)] * 3
    else:
        out_shape, scratch = carry, []
    return list(
        pl.pallas_call(
            functools.partial(attend_kernel, len(arrays), units, tiles, first, last, rider),
            out_shape=out_shape,
            in_specs=[vmem()] * len(inputs),
            out_specs=[vmem()] * len(out_shape),
            scratch_shapes=scratch,
            input_output_aliases=aliases,
            compiler_params=pltpu.CompilerParams(vmem_limit_bytes=20 * 1024 * 1024),
            cost_estimate=pl.CostEstimate(
                flops=4 * work * HD, bytes_accessed=1 << 20, transcendentals=work
            ),
            name="attend_last" if last else "attend",
        )(*inputs)
    )


def body(queries, keys, values, segments, basis):
    odd = lax.axis_index("y") & 1
    send0, send1, latents, energy = pl.pallas_call(
        prepare_kernel,
        out_shape=[
            rows(BLOCK + RIDER),
            rows(BLOCK + RIDER),
            jax.ShapeDtypeStruct((128, 128), jnp.bfloat16),
            jax.ShapeDtypeStruct((8, 128), jnp.float32),
        ],
        in_specs=[pl.BlockSpec(memory_space=pltpu.HBM)] * 4,
        out_specs=[vmem()] * 4,
        scratch_shapes=[
            pltpu.VMEM((128, 256), jnp.bfloat16),
            pltpu.VMEM((128, 256), jnp.bfloat16),
            pltpu.VMEM((1, 128), jnp.int32),
            pltpu.VMEM((2, 2, RANK, HD), jnp.bfloat16),
            pltpu.SemaphoreType.DMA((4,)),
        ],
        compiler_params=pltpu.CompilerParams(vmem_limit_bytes=66100000),
        name="prepare",
    )(keys, values, segments.reshape(1, 128), jnp.swapaxes(basis, 2, 3))
    kv = [lax.ppermute(array, COLUMN, to_heads(t)) for t, array in enumerate((send0, send1))]
    slices = [lax.dynamic_slice_in_dim(queries, (odd ^ t) * 1024, 1024, 1) for t in range(2)]
    q = []
    for t in range(2):
        q.append(lax.ppermute(slices[t], COLUMN, to_heads(t)))
    *kv, _, _ = lax.optimization_barrier((*kv, *slices))
    energy = added(added(energy, "c", 1), "xl", 1)

    def partner(array):
        return lax.ppermute(array, "c", [(0, 1), (1, 0)])

    def after(state, *arrays):
        state[2], *arrays = lax.optimization_barrier((state[2], *arrays))
        return arrays

    def piece(array, row, distance, other):
        return (array, row, distance, other, (None,) if distance == 9 else (0, 1))

    (own,) = small(start_kernel, [rows(HALF + RIDER)], *kv, energy)
    eight = shifted(own, 8)
    up, down = small(once_kernel, [rows(HALF + RIDER)] * 2, own, eight)
    one, seven = shifted(up, 1), shifted(down, -1)
    state = attend(
        q, [own, eight], ((piece(0, 0, 0, False), piece(1, 0, 8, False)),), None
    )

    one, seven = after(state, one, seven)
    far_up, far_down = small(
        twice_kernel, [rows(2 * HALF + 2 * RIDER), rows(2 * HALF + RIDER)], up, one, down, seven
    )
    two_three, six_five = shifted(far_up, 2), shifted(far_down, -2)
    other_zero_one, other_eight_seven = partner(far_up), partner(far_down)
    state = attend(
        None, [one, seven], ((piece(0, 0, 1, False), piece(1, 0, 7, False)),), state
    )
    state = attend(
        None,
        [other_zero_one, other_eight_seven],
        (
            (piece(0, 0, 0, True), piece(0, HALF, 1, True)),
            (piece(1, 0, 8, True), piece(1, HALF, 7, True)),
        ),
        state,
    )

    (two_three,) = after(state, two_three)
    (three_tail,) = small(tail_kernel, [rows(HALF + BLOCK + RIDER)], two_three, eight)
    four = shifted(three_tail, 1)
    other_two_three = partner(two_three)
    state = attend(
        None, [two_three], ((piece(0, 0, 2, False), piece(0, HALF, 3, False)),), state
    )

    (six_five,) = after(state, six_five)
    other_six_five = partner(six_five)
    state = attend(
        None,
        [other_two_three, six_five],
        (
            (piece(0, 0, 2, True), piece(0, HALF, 3, True)),
            (piece(1, 0, 6, False), piece(1, HALF, 5, False)),
        ),
        state,
    )

    (four,) = after(state, four)
    four, energy = small(
        total_kernel,
        [rows(HALF + BLOCK + RIDER), jax.ShapeDtypeStruct((RIDER, 128), jnp.float32)],
        four,
        up,
        one,
        seven,
        two_three,
        six_five,
    )
    other_four = partner(four)
    energy = lax.ppermute(energy, "y", [(i, i ^ 2) for i in range(4)])
    state = attend(
        None, [other_six_five], ((piece(0, 0, 6, True), piece(0, HALF, 5, True)),), state
    )
    units = (
        (piece(1, 0, 4, False), piece(1, HALF, 9, False)),
        (piece(0, 0, 4, True), piece(0, HALF, 9, True)),
    )
    back = []
    for t in range(2):
        (mixed,) = attend(
            None, [other_four, four], units, state, t, HALF + BLOCK, energy
        )
        back.append(lax.ppermute(mixed, COLUMN, [(d, s) for s, d in to_heads(t)]))
    attention, captured, share = small(
        finish_kernel,
        [
            jax.ShapeDtypeStruct((128, 2048), jnp.bfloat16),
            jax.ShapeDtypeStruct((4, RANK, RANK), jnp.float32),
            jax.ShapeDtypeStruct((2, 2), jnp.float32),
        ],
        *back,
    )
    return (attention, latents, captured.reshape(2, 2, RANK, RANK), share)


def solution(mesh):
    torus = Mesh(mesh.devices.reshape(2, 8, 4, 2, 2), ("a", "z", "y", "xl", "c"))
    in_specs = (P(SEQ, KV), P(SEQ, KV), P(SEQ, KV), P(SEQ), P(KV, None, None, None))
    out_specs = (P(SEQ, KV), P(SEQ, KV), P(KV, None, None, None), P(KV, None))

    return jax.shard_map(body, mesh=torus, in_specs=in_specs, out_specs=out_specs, check_vma=False)
```

profile of v0, /device:TPU:7, one launch (start us, length us, event | category | flops | bytes accessed | tf_op | source)
XLA Modules:
  0.0 83.1 jit_solution(9961445179509100158)
XLA Ops:
  0.6 2.1 %prepare.1 = (bf16[176,256]{1,0:T(8,128)(2,1)}, bf16[176,256]{1,0:T(8,128)(2,1)}, bf16[128,128]{1,0:T(8,128)(2,1)}, f32[8,128]{1,0:T(8,128)}) custom-call(bf16[128,256]{1,0:T(8,128)(2,1)} %keys_hbm.1, bf16[128,256]{1,0:T(8,128)(2,1)} %values_hbm.1, s32[1,128]{1,0:T(1,128)} %bitcast.4, bf16[2,2,32,128]{3,2,1,0:T(8,128)(2,1)} %bitcast.3), custom_call_target="tpu_custom_call" | custom-call | tf_op jit(solution)/shard_map/prepare/pallas_call | solution.py:441
  2.8 0.8 collective-permute-start.2
  3.5 4.7 %collective-permute-start = (bf16[176,256]{1,0:T(8,128)(2,1)}, bf16[176,256]{1,0:T(8,128)(2,1)S(1)}, u32[]{:S(2)}, u32[]{:S(2)}) collective-permute-start(bf16[176,256]{1,0:T(8,128)(2,1)} %get-tuple-element.58), channel_id=1, source_target_pairs={{0,0},{1,8},{4,4},{5,12},{8,1},{9,9},{12,5},{13,13},{2,2},{3,10},{... | collective-permute-start | bytes 270344 | tf_op jit(solution)/shard_map/ppermute | solution.py:461
  8.3 1.2 %collective-permute-start.1 = (bf16[176,256]{1,0:T(8,128)(2,1)}, bf16[176,256]{1,0:T(8,128)(2,1)S(1)}, u32[]{:S(2)}, u32[]{:S(2)}) collective-permute-start(bf16[176,256]{1,0:T(8,128)(2,1)} %get-tuple-element.59), channel_id=1, source_target_pairs={{0,4},{1,12},{4,0},{5,8},{8,5},{9,13},{12,1},{13,9},{2,6},{3,14},{... | collective-permute-start | bytes 270344 | tf_op jit(solution)/shard_map/ppermute | solution.py:461
  9.5 0.0 collective-permute-done.2
  9.5 0.7 copy-done
  10.2 0.5 collective-permute-start.3
  10.7 1.1 %constant_dynamic-slice_fusion = (bf16[128,1024]{1,0:T(8,128)(2,1)S(1)}, bf16[128,1024]{1,0:T(8,128)(2,1)S(1)}) fusion(bf16[128,2048]{1,0:T(8,128)(2,1)} %param.5, s32[]{:T(128)S(6)} %select_n.7, s32[]{:T(128)S(6)} %select_n.6), kind=kLoop, calls=%fused_computation | loop fusion | bytes 1048584 | tf_op jit(solution)/shard_map/dynamic_slice | solution.py:462
  11.8 0.8 %collective-permute-done.3 = f32[8,128]{1,0:T(8,128)S(1)} collective-permute-done((f32[8,128]{1,0:T(8,128)S(1)}, f32[8,128]{1,0:T(8,128)S(1)}, u32[]{:S(2)}, u32[]{:S(2)}) %collective-permute-start.3) | collective-permute-done | bytes 4128 | tf_op jit(solution)/shard_map/ppermute | solution.py:45
  12.7 0.0 collective-permute-done.first_ref
  12.7 1.1 %collective-permute-done.1.second_ref = bf16[176,256]{1,0:T(8,128)(2,1)S(1)} collective-permute-done((bf16[176,256]{1,0:T(8,128)(2,1)}, bf16[176,256]{1,0:T(8,128)(2,1)S(1)}, u32[]{:S(2)}, u32[]{:S(2)}) %collective-permute-start.1) | collective-permute-done | bytes 90144 | tf_op jit(solution)/shard_map/ppermute | solution.py:461
  13.7 1.2 %collective-permute-start.4 = (bf16[320,256]{1,0:T(8,128)(2,1)S(1)}, bf16[320,256]{1,0:T(8,128)(2,1)S(1)}, u32[]{:S(2)}, u32[]{:S(2)}) collective-permute-start(bf16[320,256]{1,0:T(8,128)(2,1)S(1)} %shard_map.84.own_ref.refs_2_), channel_id=1, source_target_pairs={{0,128},{16,144},{32,160},{48,176},{64,192},{80,208},{96,224},{112... | collective-permute-start | bytes 491528 | tf_op jit(solution)/shard_map/ppermute | solution.py:40
  15.0 3.6 %collective-permute-start.5 = (bf16[128,1024]{1,0:T(8,128)(2,1)S(1)}, bf16[128,1024]{1,0:T(8,128)(2,1)S(1)}, u32[]{:S(2)}, u32[]{:S(2)}) collective-permute-start(bf16[128,1024]{1,0:T(8,128)(2,1)S(1)} %get-tuple-element.113), channel_id=1, source_target_pairs={{0,0},{1,8},{4,4},{5,12},{8,1},{9,9},{12,5},{13,13},{2,2},{3,10},{... | collective-permute-start | bytes 786440 | tf_op jit(solution)/shard_map/ppermute | solution.py:465
  18.6 0.7 collective-permute-start.6
  19.2 0.3 collective-permute-done.4.eight_ref.refs_3_
  19.5 1.7 %collective-permute-start.7 = (bf16[320,256]{1,0:T(8,128)(2,1)S(1)}, bf16[320,256]{1,0:T(8,128)(2,1)S(1)}, u32[]{:S(2)}, u32[]{:S(2)}) collective-permute-start(bf16[320,256]{1,0:T(8,128)(2,1)S(1)} %get-tuple-element.63.up_ref), channel_id=1, source_target_pairs={{0,16},{16,32},{32,48},{48,64},{64,80},{80,96},{96,112},{112,128},... | collective-permute-start | bytes 491528 | tf_op jit(solution)/shard_map/ppermute | solution.py:40
  21.2 5.3 %collective-permute-start.8 = (bf16[320,256]{1,0:T(8,128)(2,1)S(1)}, bf16[320,256]{1,0:T(8,128)(2,1)S(1)}, u32[]{:S(2)}, u32[]{:S(2)}) collective-permute-start(bf16[320,256]{1,0:T(8,128)(2,1)S(1)} %get-tuple-element.65.down_ref), channel_id=1, source_target_pairs={{0,240},{16,0},{32,16},{48,32},{64,48},{80,64},{96,80},{112,96},{1... | collective-permute-start | bytes 491528 | tf_op jit(solution)/shard_map/ppermute | solution.py:40
  26.6 0.0 collective-permute-done.5.refs_0_
  26.6 0.6 collective-permute-done.6.refs_1_
  27.2 2.1 %attend.6 = (bf16[2048,128]{1,0:T(8,128)(2,1)S(1)}, f32[32,128]{1,0:T(8,128)S(1)}, f32[2048,128]{1,0:T(8,128)S(1)}, f32[2048,128]{1,0:T(8,128)S(1)}, f32[2048,128]{1,0:T(8,128)S(1)}) custom-call(bf16[128,1024]{1,0:T(8,128)(2,1)S(1)} %collective-permute-done.5.refs_0_, bf16[128,1024]{1,0:T(8,128)(2,1)S(1)} %collective-permute-done.6.refs_1_, ...), custom_call_target="tpu_custom_call" | custom-call | flops 536870912 | bytes 1048576 | tf_op jit(solution)/shard_map/attend/pallas_call | solution.py:423
  29.3 0.0 collective-permute-done.8.seven_ref.refs_1_
  29.3 0.1 shard_map.86
  29.4 0.1 collective-permute-start.9
  29.5 0.5 collective-permute-start.10
  30.0 2.7 %collective-permute-start.11 = (bf16[640,256]{1,0:T(8,128)(2,1)S(1)}, bf16[640,256]{1,0:T(8,128)(2,1)S(1)}, u32[]{:S(2)}, u32[]{:S(2)}) collective-permute-start(bf16[640,256]{1,0:T(8,128)(2,1)S(1)} %get-tuple-element.68), channel_id=1, source_target_pairs={{0,32},{16,48},{32,64},{48,80},{64,96},{80,112},{96,128},{112,144}... | collective-permute-start | bytes 983048 | tf_op jit(solution)/shard_map/ppermute | solution.py:40
  32.7 4.6 %collective-permute-start.13 = (bf16[608,256]{1,0:T(8,128)(2,1)S(1)}, bf16[608,256]{1,0:T(8,128)(2,1)S(1)}, u32[]{:S(2)}, u32[]{:S(2)}) collective-permute-start(bf16[608,256]{1,0:T(8,128)(2,1)S(1)} %get-tuple-element.69), channel_id=1, source_target_pairs={{0,224},{16,240},{32,0},{48,16},{64,32},{80,48},{96,64},{112,80},{... | collective-permute-start | bytes 933896 | tf_op jit(solution)/shard_map/ppermute | solution.py:40
  37.3 1.9 %attend.7 = (bf16[2048,128]{1,0:T(8,128)(2,1)S(1)}, f32[32,128]{1,0:T(8,128)S(1)}, f32[2048,128]{1,0:T(8,128)S(1)}, f32[2048,128]{1,0:T(8,128)S(1)}, f32[2048,128]{1,0:T(8,128)S(1)}) custom-call(bf16[320,256]{1,0:T(8,128)(2,1)S(1)} %collective-permute-done.7.one_ref.refs_0_, ...), custom_call_target="tpu_custom_call", output_to_operand_aliasing={{0}: (2, {}), {1}: (3, {}), {2}: (4, {}), {3}: (5, {}), {4}... | custom-call | flops 536870912 | bytes 1048576 | tf_op jit(solution)/shard_map/attend/pallas_call | solution.py:423
  39.2 0.0 collective-permute-done.9.refs_0_
  39.2 2.1 %attend.8 = (bf16[2048,128]{1,0:T(8,128)(2,1)S(1)}, f32[32,128]{1,0:T(8,128)S(1)}, f32[2048,128]{1,0:T(8,128)S(1)}, f32[2048,128]{1,0:T(8,128)S(1)}, f32[2048,128]{1,0:T(8,128)S(1)}) custom-call(bf16[640,256]{1,0:T(8,128)(2,1)S(1)} %collective-permute-done.9.refs_0_, ...), custom_call_target="tpu_custom_call", output_to_operand_aliasing={{0}: (2, {}), {1}: (3, {}), {2}: (4, {}), {3}: (5, {}), {4}... | custom-call | flops 1073741824 | bytes 1048576 | tf_op jit(solution)/shard_map/attend/pallas_call | solution.py:423
  41.4 5.9 %collective-permute-done.11.refs_0_.two_three_ref = bf16[640,256]{1,0:T(8,128)(2,1)S(1)} collective-permute-done((bf16[640,256]{1,0:T(8,128)(2,1)S(1)}, bf16[640,256]{1,0:T(8,128)(2,1)S(1)}, u32[]{:S(2)}, u32[]{:S(2)}) %collective-permute-start.11) | collective-permute-done | bytes 327712 | tf_op jit(solution)/shard_map/ppermute | solution.py:40
  47.3 1.4 %collective-permute-start.12 = (bf16[640,256]{1,0:T(8,128)(2,1)S(1)}, bf16[640,256]{1,0:T(8,128)(2,1)S(1)}, u32[]{:S(2)}, u32[]{:S(2)}) collective-permute-start(bf16[640,256]{1,0:T(8,128)(2,1)S(1)} %collective-permute-done.11.refs_0_.two_three_ref), channel_id=1, source_target_pairs={{0,1},{1,0},{2,3},{3,2},{4,5},{5,4},{6,7},{7,6},{8,9},{9,8},{10,11... | collective-permute-start | bytes 983048 | tf_op jit(solution)/shard_map/ppermute | solution.py:470
  48.7 5.1 %collective-permute-start.14 = (bf16[464,256]{1,0:T(8,128)(2,1)S(1)}, bf16[464,256]{1,0:T(8,128)(2,1)S(1)}, u32[]{:S(2)}, u32[]{:S(2)}) collective-permute-start(bf16[464,256]{1,0:T(8,128)(2,1)S(1)} %shard_map.87), channel_id=1, source_target_pairs={{0,16},{16,32},{32,48},{48,64},{64,80},{80,96},{96,112},{112,128},... | collective-permute-start | bytes 712712 | tf_op jit(solution)/shard_map/ppermute | solution.py:40
  53.8 1.9 %attend.9 = (bf16[2048,128]{1,0:T(8,128)(2,1)S(1)}, f32[32,128]{1,0:T(8,128)S(1)}, f32[2048,128]{1,0:T(8,128)S(1)}, f32[2048,128]{1,0:T(8,128)S(1)}, f32[2048,128]{1,0:T(8,128)S(1)}) custom-call(bf16[640,256]{1,0:T(8,128)(2,1)S(1)} %collective-permute-done.11.refs_0_.two_three_ref, ...), custom_call_target="tpu_custom_call", output_to_operand_aliasing={{0}: (1, {}), {1}: (2, {}), {2}: (3, {}), {3}: (4, {}), {4}... | custom-call | flops 536870912 | bytes 1048576 | tf_op jit(solution)/shard_map/attend/pallas_call | solution.py:423
  55.7 0.0 collective-permute-done.13.refs_1_.six_five_ref
  55.7 0.4 collective-permute-start.16
  56.1 3.7 %attend.10 = (bf16[2048,128]{1,0:T(8,128)(2,1)S(1)}, f32[32,128]{1,0:T(8,128)S(1)}, f32[2048,128]{1,0:T(8,128)S(1)}, f32[2048,128]{1,0:T(8,128)S(1)}, f32[2048,128]{1,0:T(8,128)S(1)}) custom-call(bf16[640,256]{1,0:T(8,128)(2,1)S(1)} %collective-permute-done.12.refs_0_, ...), custom_call_target="tpu_custom_call", output_to_operand_aliasing={{0}: (2, {}), {1}: (3, {}), {2}: (4, {}), {3}: (5, {}), {4}... | custom-call | flops 1073741824 | bytes 1048576 | tf_op jit(solution)/shard_map/attend/pallas_call | solution.py:423
  59.8 1.0 %collective-permute-done.14.four_ref = bf16[464,256]{1,0:T(8,128)(2,1)S(1)} collective-permute-done((bf16[464,256]{1,0:T(8,128)(2,1)S(1)}, bf16[464,256]{1,0:T(8,128)(2,1)S(1)}, u32[]{:S(2)}, u32[]{:S(2)}) %collective-permute-start.14) | collective-permute-done | bytes 237600 | tf_op jit(solution)/shard_map/ppermute | solution.py:40
  60.9 0.7 collective-permute-start.15
  61.5 1.5 %collective-permute-start.17 = (f32[32,128]{1,0:T(8,128)S(1)}, f32[32,128]{1,0:T(8,128)S(1)}, u32[]{:S(2)}, u32[]{:S(2)}) collective-permute-start(f32[32,128]{1,0:T(8,128)S(1)} %get-tuple-element.107), channel_id=1, source_target_pairs={{0,8},{4,12},{8,0},{12,4},{1,9},{5,13},{9,1},{13,5},{2,10},{6,14},... | collective-permute-start | bytes 49160 | tf_op jit(solution)/shard_map/ppermute | solution.py:538
  63.1 0.4 attend.11
  63.5 2.2 %collective-permute-done.17.refs_7_ = f32[32,128]{1,0:T(8,128)S(1)} collective-permute-done((f32[32,128]{1,0:T(8,128)S(1)}, f32[32,128]{1,0:T(8,128)S(1)}, u32[]{:S(2)}, u32[]{:S(2)}) %collective-permute-start.17) | collective-permute-done | bytes 16416 | tf_op jit(solution)/shard_map/ppermute | solution.py:538
  65.6 2.0 %attend_last.3 = bf16[144,1024]{1,0:T(8,128)(2,1)S(1)} custom-call(bf16[464,256]{1,0:T(8,128)(2,1)S(1)} %collective-permute-done.15.refs_0_, bf16[464,256]{1,0:T(8,128)(2,1)S(1)} %get-tuple-element.96.refs_1_, bf16[2048,128]{1,0:T(8,128)(2,1)S(1)} %get-tuple-element.102.refs_2_, f32[32,128]{1,0:T(8,128)S(1)} %get-tuple-element.103.refs_3_, ...), custom_call_target="tpu_custom_call" | custom-call | flops 402653184 | bytes 1048576 | tf_op jit(solution)/shard_map/attend_last/pallas_call | solution.py:423
  67.6 3.1 %collective-permute-start.19 = (bf16[144,1024]{1,0:T(8,128)(2,1)S(1)}, bf16[144,1024]{1,0:T(8,128)(2,1)S(1)}, u32[]{:S(2)}, u32[]{:S(2)}) collective-permute-start(bf16[144,1024]{1,0:T(8,128)(2,1)S(1)} %attend_last.3), channel_id=1, source_target_pairs={{4,0},{12,1},{0,4},{8,5},{5,8},{13,9},{1,12},{9,13},{6,2},{14,3},{... | collective-permute-start | bytes 884744 | tf_op jit(solution)/shard_map/ppermute | solution.py:551
  70.7 2.0 %attend_last.2 = bf16[144,1024]{1,0:T(8,128)(2,1)S(1)} custom-call(bf16[464,256]{1,0:T(8,128)(2,1)S(1)} %collective-permute-done.15.refs_0_, bf16[464,256]{1,0:T(8,128)(2,1)S(1)} %get-tuple-element.96.refs_1_, bf16[2048,128]{1,0:T(8,128)(2,1)S(1)} %get-tuple-element.102.refs_2_, f32[32,128]{1,0:T(8,128)S(1)} %get-tuple-element.103.refs_3_, ...), custom_call_target="tpu_custom_call" | custom-call | flops 402653184 | bytes 1048576 | tf_op jit(solution)/shard_map/attend_last/pallas_call | solution.py:423
  72.7 1.9 %collective-permute-start.18 = (bf16[144,1024]{1,0:T(8,128)(2,1)S(1)}, bf16[144,1024]{1,0:T(8,128)(2,1)S(1)}, u32[]{:S(2)}, u32[]{:S(2)}) collective-permute-start(bf16[144,1024]{1,0:T(8,128)(2,1)S(1)} %attend_last.2), channel_id=1, source_target_pairs={{0,0},{8,1},{4,4},{12,5},{1,8},{9,9},{5,12},{13,13},{2,2},{10,3},{... | collective-permute-start | bytes 884744 | tf_op jit(solution)/shard_map/ppermute | solution.py:551
  74.6 0.5 collective-permute-done.19.second_ref
  75.1 7.1 %collective-permute-done.18.first_ref = bf16[144,1024]{1,0:T(8,128)(2,1)S(1)} collective-permute-done((bf16[144,1024]{1,0:T(8,128)(2,1)S(1)}, bf16[144,1024]{1,0:T(8,128)(2,1)S(1)}, u32[]{:S(2)}, u32[]{:S(2)}) %collective-permute-start.18) | collective-permute-done | bytes 294944 | tf_op jit(solution)/shard_map/ppermute | solution.py:551
  82.2 0.8 %shard_map.89 = (bf16[128,2048]{1,0:T(8,128)(2,1)}, f32[4,32,32]{2,1,0:T(8,128)}, f32[2,2]{1,0:T(2,128)}) custom-call(bf16[144,1024]{1,0:T(8,128)(2,1)S(1)} %collective-permute-done.18.first_ref, bf16[144,1024]{1,0:T(8,128)(2,1)S(1)} %collective-permute-done.19.second_ref), custom_call_target="tpu_custom_call" | custom-call | flops 1048576 | bytes 262144 | tf_op jit(solution)/shard_map/pallas_call | solution.py:387
  (12 shorter events, 0.1 us)
Async XLA Ops:
  2.8 6.7 %collective-permute-start.2 = (f32[8,128]{1,0:T(8,128)}, f32[8,128]{1,0:T(8,128)S(1)}, u32[]{:S(2)}, u32[]{:S(2)}) collective-permute-start(f32[8,128]{1,0:T(8,128)} %get-tuple-element.62), channel_id=1, source_target_pairs={{0,1},{1,0},{2,3},{3,2},{4,5},{5,4},{6,7},{7,6},{8,9},{9,8},{10,11... | collective-permute-start | bytes 12296 | tf_op jit(solution)/shard_map/ppermute | solution.py:45
  3.5 9.1 %collective-permute-start = (bf16[176,256]{1,0:T(8,128)(2,1)}, bf16[176,256]{1,0:T(8,128)(2,1)S(1)}, u32[]{:S(2)}, u32[]{:S(2)}) collective-permute-start(bf16[176,256]{1,0:T(8,128)(2,1)} %get-tuple-element.58), channel_id=1, source_target_pairs={{0,0},{1,8},{4,4},{5,12},{8,1},{9,9},{12,5},{13,13},{2,2},{3,10},{... | collective-permute-start | bytes 270344 | tf_op jit(solution)/shard_map/ppermute | solution.py:461
  8.3 5.5 %collective-permute-start.1 = (bf16[176,256]{1,0:T(8,128)(2,1)}, bf16[176,256]{1,0:T(8,128)(2,1)S(1)}, u32[]{:S(2)}, u32[]{:S(2)}) collective-permute-start(bf16[176,256]{1,0:T(8,128)(2,1)} %get-tuple-element.59), channel_id=1, source_target_pairs={{0,4},{1,12},{4,0},{5,8},{8,5},{9,13},{12,1},{13,9},{2,6},{3,14},{... | collective-permute-start | bytes 270344 | tf_op jit(solution)/shard_map/ppermute | solution.py:461
  9.5 0.7 copy-start
  10.2 2.5 %collective-permute-start.3 = (f32[8,128]{1,0:T(8,128)S(1)}, f32[8,128]{1,0:T(8,128)S(1)}, u32[]{:S(2)}, u32[]{:S(2)}) collective-permute-start(f32[8,128]{1,0:T(8,128)S(1)} %add.14), channel_id=1, source_target_pairs={{0,2},{2,0},{1,3},{3,1},{4,6},{6,4},{5,7},{7,5},{8,10},{10,8},{9,1... | collective-permute-start | bytes 12296 | tf_op jit(solution)/shard_map/ppermute | solution.py:45
  13.7 5.8 %collective-permute-start.4 = (bf16[320,256]{1,0:T(8,128)(2,1)S(1)}, bf16[320,256]{1,0:T(8,128)(2,1)S(1)}, u32[]{:S(2)}, u32[]{:S(2)}) collective-permute-start(bf16[320,256]{1,0:T(8,128)(2,1)S(1)} %shard_map.84.own_ref.refs_2_), channel_id=1, source_target_pairs={{0,128},{16,144},{32,160},{48,176},{64,192},{80,208},{96,224},{112... | collective-permute-start | bytes 491528 | tf_op jit(solution)/shard_map/ppermute | solution.py:40
  15.0 11.6 %collective-permute-start.5 = (bf16[128,1024]{1,0:T(8,128)(2,1)S(1)}, bf16[128,1024]{1,0:T(8,128)(2,1)S(1)}, u32[]{:S(2)}, u32[]{:S(2)}) collective-permute-start(bf16[128,1024]{1,0:T(8,128)(2,1)S(1)} %get-tuple-element.113), channel_id=1, source_target_pairs={{0,0},{1,8},{4,4},{5,12},{8,1},{9,9},{12,5},{13,13},{2,2},{3,10},{... | collective-permute-start | bytes 786440 | tf_op jit(solution)/shard_map/ppermute | solution.py:465
  18.6 8.7 %collective-permute-start.6 = (bf16[128,1024]{1,0:T(8,128)(2,1)S(1)}, bf16[128,1024]{1,0:T(8,128)(2,1)S(1)}, u32[]{:S(2)}, u32[]{:S(2)}) collective-permute-start(bf16[128,1024]{1,0:T(8,128)(2,1)S(1)} %get-tuple-element.112), channel_id=1, source_target_pairs={{0,4},{1,12},{4,0},{5,8},{8,5},{9,13},{12,1},{13,9},{2,6},{3,14},{... | collective-permute-start | bytes 786440 | tf_op jit(solution)/shard_map/ppermute | solution.py:465
  19.5 9.8 %collective-permute-start.7 = (bf16[320,256]{1,0:T(8,128)(2,1)S(1)}, bf16[320,256]{1,0:T(8,128)(2,1)S(1)}, u32[]{:S(2)}, u32[]{:S(2)}) collective-permute-start(bf16[320,256]{1,0:T(8,128)(2,1)S(1)} %get-tuple-element.63.up_ref), channel_id=1, source_target_pairs={{0,16},{16,32},{32,48},{48,64},{64,80},{80,96},{96,112},{112,128},... | collective-permute-start | bytes 491528 | tf_op jit(solution)/shard_map/ppermute | solution.py:40
  21.2 8.1 %collective-permute-start.8 = (bf16[320,256]{1,0:T(8,128)(2,1)S(1)}, bf16[320,256]{1,0:T(8,128)(2,1)S(1)}, u32[]{:S(2)}, u32[]{:S(2)}) collective-permute-start(bf16[320,256]{1,0:T(8,128)(2,1)S(1)} %get-tuple-element.65.down_ref), channel_id=1, source_target_pairs={{0,240},{16,0},{32,16},{48,32},{64,48},{80,64},{96,80},{112,96},{1... | collective-permute-start | bytes 491528 | tf_op jit(solution)/shard_map/ppermute | solution.py:40
  29.4 9.8 %collective-permute-start.9 = (bf16[640,256]{1,0:T(8,128)(2,1)S(1)}, bf16[640,256]{1,0:T(8,128)(2,1)S(1)}, u32[]{:S(2)}, u32[]{:S(2)}) collective-permute-start(bf16[640,256]{1,0:T(8,128)(2,1)S(1)} %get-tuple-element.68), channel_id=1, source_target_pairs={{0,1},{1,0},{2,3},{3,2},{4,5},{5,4},{6,7},{7,6},{8,9},{9,8},{10,11... | collective-permute-start | bytes 983048 | tf_op jit(solution)/shard_map/ppermute | solution.py:470
  29.5 9.7 %collective-permute-start.10 = (bf16[608,256]{1,0:T(8,128)(2,1)S(1)}, bf16[608,256]{1,0:T(8,128)(2,1)S(1)}, u32[]{:S(2)}, u32[]{:S(2)}) collective-permute-start(bf16[608,256]{1,0:T(8,128)(2,1)S(1)} %get-tuple-element.69), channel_id=1, source_target_pairs={{0,1},{1,0},{2,3},{3,2},{4,5},{5,4},{6,7},{7,6},{8,9},{9,8},{10,11... | collective-permute-start | bytes 933896 | tf_op jit(solution)/shard_map/ppermute | solution.py:470
  30.0 17.3 %collective-permute-start.11 = (bf16[640,256]{1,0:T(8,128)(2,1)S(1)}, bf16[640,256]{1,0:T(8,128)(2,1)S(1)}, u32[]{:S(2)}, u32[]{:S(2)}) collective-permute-start(bf16[640,256]{1,0:T(8,128)(2,1)S(1)} %get-tuple-element.68), channel_id=1, source_target_pairs={{0,32},{16,48},{32,64},{48,80},{64,96},{80,112},{96,128},{112,144}... | collective-permute-start | bytes 983048 | tf_op jit(solution)/shard_map/ppermute | solution.py:40
  32.7 23.0 %collective-permute-start.13 = (bf16[608,256]{1,0:T(8,128)(2,1)S(1)}, bf16[608,256]{1,0:T(8,128)(2,1)S(1)}, u32[]{:S(2)}, u32[]{:S(2)}) collective-permute-start(bf16[608,256]{1,0:T(8,128)(2,1)S(1)} %get-tuple-element.69), channel_id=1, source_target_pairs={{0,224},{16,240},{32,0},{48,16},{64,32},{80,48},{96,64},{112,80},{... | collective-permute-start | bytes 933896 | tf_op jit(solution)/shard_map/ppermute | solution.py:40
  47.3 8.8 %collective-permute-start.12 = (bf16[640,256]{1,0:T(8,128)(2,1)S(1)}, bf16[640,256]{1,0:T(8,128)(2,1)S(1)}, u32[]{:S(2)}, u32[]{:S(2)}) collective-permute-start(bf16[640,256]{1,0:T(8,128)(2,1)S(1)} %collective-permute-done.11.refs_0_.two_three_ref), channel_id=1, source_target_pairs={{0,1},{1,0},{2,3},{3,2},{4,5},{5,4},{6,7},{7,6},{8,9},{9,8},{10,11... | collective-permute-start | bytes 983048 | tf_op jit(solution)/shard_map/ppermute | solution.py:470
  48.7 12.2 %collective-permute-start.14 = (bf16[464,256]{1,0:T(8,128)(2,1)S(1)}, bf16[464,256]{1,0:T(8,128)(2,1)S(1)}, u32[]{:S(2)}, u32[]{:S(2)}) collective-permute-start(bf16[464,256]{1,0:T(8,128)(2,1)S(1)} %shard_map.87), channel_id=1, source_target_pairs={{0,16},{16,32},{32,48},{48,64},{64,80},{80,96},{96,112},{112,128},... | collective-permute-start | bytes 712712 | tf_op jit(solution)/shard_map/ppermute | solution.py:40
  55.7 7.3 %collective-permute-start.16 = (bf16[608,256]{1,0:T(8,128)(2,1)S(1)}, bf16[608,256]{1,0:T(8,128)(2,1)S(1)}, u32[]{:S(2)}, u32[]{:S(2)}) collective-permute-start(bf16[608,256]{1,0:T(8,128)(2,1)S(1)} %collective-permute-done.13.refs_1_.six_five_ref), channel_id=1, source_target_pairs={{0,1},{1,0},{2,3},{3,2},{4,5},{5,4},{6,7},{7,6},{8,9},{9,8},{10,11... | collective-permute-start | bytes 933896 | tf_op jit(solution)/shard_map/ppermute | solution.py:470
  60.9 4.8 %collective-permute-start.15 = (bf16[464,256]{1,0:T(8,128)(2,1)S(1)}, bf16[464,256]{1,0:T(8,128)(2,1)S(1)}, u32[]{:S(2)}, u32[]{:S(2)}) collective-permute-start(bf16[464,256]{1,0:T(8,128)(2,1)S(1)} %get-tuple-element.96.refs_1_), channel_id=1, source_target_pairs={{0,1},{1,0},{2,3},{3,2},{4,5},{5,4},{6,7},{7,6},{8,9},{9,8},{10,11... | collective-permute-start | bytes 712712 | tf_op jit(solution)/shard_map/ppermute | solution.py:470
  61.5 4.1 %collective-permute-start.17 = (f32[32,128]{1,0:T(8,128)S(1)}, f32[32,128]{1,0:T(8,128)S(1)}, u32[]{:S(2)}, u32[]{:S(2)}) collective-permute-start(f32[32,128]{1,0:T(8,128)S(1)} %get-tuple-element.107), channel_id=1, source_target_pairs={{0,8},{4,12},{8,0},{12,4},{1,9},{5,13},{9,1},{13,5},{2,10},{6,14},... | collective-permute-start | bytes 49160 | tf_op jit(solution)/shard_map/ppermute | solution.py:538
  67.6 7.5 %collective-permute-start.19 = (bf16[144,1024]{1,0:T(8,128)(2,1)S(1)}, bf16[144,1024]{1,0:T(8,128)(2,1)S(1)}, u32[]{:S(2)}, u32[]{:S(2)}) collective-permute-start(bf16[144,1024]{1,0:T(8,128)(2,1)S(1)} %attend_last.3), channel_id=1, source_target_pairs={{4,0},{12,1},{0,4},{8,5},{5,8},{13,9},{1,12},{9,13},{6,2},{14,3},{... | collective-permute-start | bytes 884744 | tf_op jit(solution)/shard_map/ppermute | solution.py:551
  72.7 9.5 %collective-permute-start.18 = (bf16[144,1024]{1,0:T(8,128)(2,1)S(1)}, bf16[144,1024]{1,0:T(8,128)(2,1)S(1)}, u32[]{:S(2)}, u32[]{:S(2)}) collective-permute-start(bf16[144,1024]{1,0:T(8,128)(2,1)S(1)} %attend_last.2), channel_id=1, source_target_pairs={{0,0},{8,1},{4,4},{12,5},{1,8},{9,9},{5,12},{13,13},{2,2},{10,3},{... | collective-permute-start | bytes 884744 | tf_op jit(solution)/shard_map/ppermute | solution.py:551
where the time goes:
time: 83.3 us; the launch traced here: 83.1 us
  starting transfers between devices  41.8 us (50%)
  waiting for transfers between devices  19.5 us (23%)
  Pallas kernels  19.2 us (23%)
  local copies, waits for them, and re-layouts  1.75 us (2%)
    ppermute x6, starting transfers between devices, shifted(): lax.ppermute(array, RING, [(i, (i + by) % SLABS) for i in range(SLABS)])  20.7 us
    pallas_call x8, Pallas kernels, attend(): pl.pallas_call(functools.partial(attend_kernel, len(arrays), units, tiles...  16.1 us
    ppermute x2, waiting for transfers between devices, body(): back.append(lax.ppermute(mixed, COLUMN, [(d, s) for s, d in to_heads(t)]))  7.62 us
    ppermute x6, waiting for transfers between devices, shifted(): lax.ppermute(array, RING, [(i, (i + by) % SLABS) for i in range(SLABS)])  7.2 us
    ppermute x2, starting transfers between devices, body(): lax.ppermute(array, COLUMN, to_heads(t))  5.97 us
    ppermute x2, starting transfers between devices, body(): back.append(lax.ppermute(mixed, COLUMN, [(d, s) for s, d in to_heads(t)]))  4.98 us
    ppermute x2, starting transfers between devices, body(): q.append(lax.ppermute(slices[t], COLUMN, to_heads(t)))  4.29 us
    ppermute x5, starting transfers between devices, partner(): return lax.ppermute(array, 'c', [(0, 1), (1, 0)])  2.99 us
  transfers between devices with their start and end apart: 20, of which 9 were waited for; matrix products, arithmetic and copies ran while one was open for 1% of the time, Pallas kernels for 17%

commit v1 on v0

--- a/solution.py
+++ b/solution.py
@@ -178,45 +178,40 @@
     put(out_ref, HALF, got(first_ref, BLOCK) + got(second_ref, BLOCK) + energy)
 
 
-def once_kernel(own_ref, eight_ref, up_ref, down_ref):
+def once_kernel(own_ref, eight_ref, up_ref, down_ref, both_ref):
     both = got(own_ref, HALF) + got(eight_ref, HALF)
     up_ref[0:HALF, :] = own_ref[0:HALF, :]
     down_ref[0:HALF, :] = eight_ref[0:HALF, :]
     put(up_ref, HALF, both)
     put(down_ref, HALF, both)
-
-
-def twice_kernel(up_ref, one_ref, down_ref, seven_ref, far_up_ref, far_down_ref):
-    far_up_ref[0:HALF, :] = up_ref[0:HALF, :]
-    far_up_ref[HALF : 2 * HALF, :] = one_ref[0:HALF, :]
-    far_up_ref[2 * HALF : 2 * HALF + RIDER, :] = up_ref[HALF : HALF + RIDER, :]
-    far_up_ref[2 * HALF + RIDER : 2 * HALF + 2 * RIDER, :] = one_ref[HALF : HALF + RIDER, :]
-    far_down_ref[0:HALF, :] = down_ref[0:HALF, :]
-    far_down_ref[HALF : 2 * HALF, :] = seven_ref[0:HALF, :]
-    put(far_down_ref, 2 * HALF, got(down_ref, HALF) + got(seven_ref, HALF))
-
-
-def tail_kernel(two_three_ref, eight_ref, out_ref):
-    out_ref[0:HALF, :] = two_three_ref[HALF : 2 * HALF, :]
     for odd in range(2):
 
         @pl.when(place()[2] == odd)
         def _(odd=odd):
             row = (1 - odd) * BLOCK
-            out_ref[HALF : HALF + BLOCK, :] = eight_ref[row : row + BLOCK, :]
-
-    out_ref[HALF + BLOCK : HALF + BLOCK + RIDER, :] = two_three_ref[
-        2 * HALF + RIDER : 2 * HALF + 2 * RIDER, :
-    ]
-
-
-def total_kernel(four_ref, up_ref, one_ref, seven_ref, two_three_ref, six_five_ref, out_ref, energy_ref):
-    at = HALF + BLOCK
-    out_ref[0:at, :] = four_ref[0:at, :]
-    total = got(up_ref, HALF) + got(one_ref, HALF) + got(seven_ref, HALF)
-    total += got(two_three_ref, 2 * HALF) + got(two_three_ref, 2 * HALF + RIDER)
-    total += got(six_five_ref, 2 * HALF) + got(four_ref, at)
-    put(out_ref, at, total)
+            up_ref[HALF + RIDER : HALF + RIDER + BLOCK, :] = eight_ref[row : row + BLOCK, :]
+
+    both_ref[0:HALF, :] = own_ref[0:HALF, :]
+    both_ref[HALF : 2 * HALF, :] = eight_ref[0:HALF, :]
+
+
+def split_kernel(one_ref, seven_ref, next_ref, both_ref):
+    next_ref[...] = one_ref[0 : HALF + RIDER, :]
+    both_ref[0:HALF, :] = one_ref[0:HALF, :]
+    both_ref[HALF : 2 * HALF, :] = seven_ref[0:HALF, :]
+    both_ref[2 * HALF : 2 * HALF + BLOCK, :] = one_ref[HALF + RIDER : HALF + RIDER + BLOCK, :]
+
+
+def pair_kernel(first_ref, second_ref, both_ref):
+    both_ref[0:HALF, :] = first_ref[0:HALF, :]
+    both_ref[HALF : 2 * HALF, :] = second_ref[0:HALF, :]
+
+
+def total_kernel(*refs):
+    *terms, out_ref, energy_ref = refs
+    out_ref[0:HALF, :] = terms[0][0:HALF, :]
+    total = functools.reduce(jnp.add, [got(ref, HALF) for ref in terms])
+    put(out_ref, HALF, total)
     lane = lax.broadcasted_iota(jnp.int32, (RIDER, 128), 1) // 64
     row = lax.broadcasted_iota(jnp.int32, (RIDER, 128), 0)
     energies = (lane == 1 - place()[2]) & ((row == 2) | (row == 3))
@@ -458,13 +453,13 @@
         compiler_params=pltpu.CompilerParams(vmem_limit_bytes=66100000),
         name="prepare",
     )(keys, values, segments.reshape(1, 128), jnp.swapaxes(basis, 2, 3))
-    kv = [lax.ppermute(array, COLUMN, to_heads(t)) for t, array in enumerate((send0, send1))]
+    kv = []
+    for t, array in enumerate((send0, send1)):
+        kv.append(lax.ppermute(array, COLUMN, to_heads(t)))
     slices = [lax.dynamic_slice_in_dim(queries, (odd ^ t) * 1024, 1024, 1) for t in range(2)]
-    q = []
-    for t in range(2):
-        q.append(lax.ppermute(slices[t], COLUMN, to_heads(t)))
-    *kv, _, _ = lax.optimization_barrier((*kv, *slices))
-    energy = added(added(energy, "c", 1), "xl", 1)
+    q = [lax.ppermute(slices[t], COLUMN, to_heads(t)) for t in range(2)]
+    energy = added(energy, "c", 1)
+    energy = added(energy, "xl", 1)
 
     def partner(array):
         return lax.ppermute(array, "c", [(0, 1), (1, 0)])
@@ -476,49 +471,54 @@
     def piece(array, row, distance, other):
         return (array, row, distance, other, (None,) if distance == 9 else (0, 1))
 
-    (own,) = small(start_kernel, [rows(HALF + RIDER)], *kv, energy)
+    message = rows(HALF + RIDER)
+    (own,) = small(start_kernel, [message], *kv, energy)
     eight = shifted(own, 8)
-    up, down = small(once_kernel, [rows(HALF + RIDER)] * 2, own, eight)
+    up, down, both = small(
+        once_kernel, [rows(HALF + RIDER + BLOCK), message, rows(2 * HALF)], own, eight
+    )
     one, seven = shifted(up, 1), shifted(down, -1)
-    state = attend(
-        q, [own, eight], ((piece(0, 0, 0, False), piece(1, 0, 8, False)),), None
-    )
-
-    one, seven = after(state, one, seven)
-    far_up, far_down = small(
-        twice_kernel, [rows(2 * HALF + 2 * RIDER), rows(2 * HALF + RIDER)], up, one, down, seven
-    )
-    two_three, six_five = shifted(far_up, 2), shifted(far_down, -2)
-    other_zero_one, other_eight_seven = partner(far_up), partner(far_down)
-    state = attend(
-        None, [one, seven], ((piece(0, 0, 1, False), piece(1, 0, 7, False)),), state
-    )
+    other_zero_eight = partner(both)
+
+    onward, both = small(split_kernel, [message, rows(2 * HALF + BLOCK)], one, seven)
+    two, six = shifted(onward, 1), shifted(seven, -1)
+    other_one_seven = partner(both)
+    own, onward = lax.optimization_barrier((own, onward))
+    state = attend(q, [own, eight], ((piece(0, 0, 0, False), piece(1, 0, 8, False)),), None)
     state = attend(
         None,
-        [other_zero_one, other_eight_seven],
+        [one, seven, other_zero_eight],
         (
-            (piece(0, 0, 0, True), piece(0, HALF, 1, True)),
-            (piece(1, 0, 8, True), piece(1, HALF, 7, True)),
+            (piece(0, 0, 1, False), piece(1, 0, 7, False)),
+            (piece(2, 0, 0, True), piece(2, HALF, 8, True)),
         ),
         state,
     )
 
-    (two_three,) = after(state, two_three)
-    (three_tail,) = small(tail_kernel, [rows(HALF + BLOCK + RIDER)], two_three, eight)
-    four = shifted(three_tail, 1)
-    other_two_three = partner(two_three)
-    state = attend(
-        None, [two_three], ((piece(0, 0, 2, False), piece(0, HALF, 3, False)),), state
-    )
-
-    (six_five,) = after(state, six_five)
-    other_six_five = partner(six_five)
+    two, six = after(state, two, six)
+    three, five = shifted(two, 1), shifted(six, -1)
+    (both,) = small(pair_kernel, [rows(2 * HALF)], two, six)
+    other_two_six = partner(both)
     state = attend(
         None,
-        [other_two_three, six_five],
+        [two, six, other_one_seven],
         (
-            (piece(0, 0, 2, True), piece(0, HALF, 3, True)),
-            (piece(1, 0, 6, False), piece(1, HALF, 5, False)),
+            (piece(0, 0, 2, False), piece(1, 0, 6, False)),
+            (piece(2, 0, 1, True), piece(2, HALF, 7, True)),
+        ),
+        state,
+    )
+
+    three, five = after(state, three, five)
+    four = shifted(three, 1)
+    (both,) = small(pair_kernel, [rows(2 * HALF)], three, five)
+    other_three_five = partner(both)
+    state = attend(
+        None,
+        [three, five, other_two_six],
+        (
+            (piece(0, 0, 3, False), piece(1, 0, 5, False)),
+            (piece(2, 0, 2, True), piece(2, HALF, 6, True)),
         ),
         state,
     )
@@ -526,27 +526,36 @@
     (four,) = after(state, four)
     four, energy = small(
         total_kernel,
-        [rows(HALF + BLOCK + RIDER), jax.ShapeDtypeStruct((RIDER, 128), jnp.float32)],
+        [message, jax.ShapeDtypeStruct((RIDER, 128), jnp.float32)],
         four,
         up,
         one,
         seven,
-        two_three,
-        six_five,
+        two,
+        six,
+        three,
+        five,
     )
     other_four = partner(four)
     energy = lax.ppermute(energy, "y", [(i, i ^ 2) for i in range(4)])
     state = attend(
-        None, [other_six_five], ((piece(0, 0, 6, True), piece(0, HALF, 5, True)),), state
-    )
-    units = (
-        (piece(1, 0, 4, False), piece(1, HALF, 9, False)),
-        (piece(0, 0, 4, True), piece(0, HALF, 9, True)),
-    )
+        None,
+        [four, one, other_one_seven, other_three_five],
+        (
+            (
+                piece(0, 0, 4, False),
+                piece(1, HALF + RIDER, 9, False),
+                piece(2, 2 * HALF, 9, True),
+            ),
+            (piece(3, 0, 3, True), piece(3, HALF, 5, True)),
+        ),
+        state,
+    )
+    units = ((piece(0, 0, 4, True),),)
     back = []
     for t in range(2):
         (mixed,) = attend(
-            None, [other_four, four], units, state, t, HALF + BLOCK, energy
+            None, [other_four, four], units, state, t, HALF, energy
         )
         back.append(lax.ppermute(mixed, COLUMN, [(d, s) for s, d in to_heads(t)]))
     attention, captured, share = small(

time: 83.3 us -> 89.7 us (1.077)
  the two profiles are of different devices: /device:TPU:7 before, /device:TPU:1 now
where the time goes in v1:
time: 89.7 us; the launch traced here: 89.5 us
  starting transfers between devices  47 us (52%)
  waiting for transfers between devices  32 us (36%)
  Pallas kernels  8.95 us (10%)
    ppermute x8, starting transfers between devices, shifted(): lax.ppermute(array, RING, [(i, (i + by) % SLABS) for i in range(SLABS)])  20.2 us
    ppermute x8, waiting for transfers between devices, shifted(): lax.ppermute(array, RING, [(i, (i + by) % SLABS) for i in range(SLABS)])  16.8 us
    ppermute x2, waiting for transfers between devices, body(): back.append(lax.ppermute(mixed, COLUMN, [(d, s) for s, d in to_heads(t)]))  8.25 us
    ppermute x2, starting transfers between devices, body(): kv.append(lax.ppermute(array, COLUMN, to_heads(t)))  6.8 us
    ppermute x2, starting transfers between devices, body(): q = [lax.ppermute(slices[t], COLUMN, to_heads(t)) for t in range(2)]  6.12 us
    pallas_call x7, Pallas kernels, attend(): pl.pallas_call(functools.partial(attend_kernel, len(arrays), units, tiles...  5.75 us
    ppermute x2, starting transfers between devices, body(): back.append(lax.ppermute(mixed, COLUMN, [(d, s) for s, d in to_heads(t)]))  5.55 us
    ppermute x5, starting transfers between devices, partner(): return lax.ppermute(array, 'c', [(0, 1), (1, 0)])  5.46 us
  transfers between devices with their start and end apart: 22, of which 11 were waited for; matrix products, arithmetic and copies ran while one was open for 1% of the time, Pallas kernels for 6%

profile of v1, /device:TPU:1, one launch (start us, length us, event | category | flops | bytes accessed | tf_op | source)
XLA Modules:
  0.0 89.5 jit_solution(11851420163356311627)
XLA Ops:
  0.6 2.2 %prepare.1 = (bf16[176,256]{1,0:T(8,128)(2,1)}, bf16[176,256]{1,0:T(8,128)(2,1)}, bf16[128,128]{1,0:T(8,128)(2,1)}, f32[8,128]{1,0:T(8,128)}) custom-call(bf16[128,256]{1,0:T(8,128)(2,1)} %keys_hbm.1, bf16[128,256]{1,0:T(8,128)(2,1)} %values_hbm.1, s32[1,128]{1,0:T(1,128)} %bitcast.4, bf16[2,2,32,128]{3,2,1,0:T(8,128)(2,1)} %bitcast.3), custom_call_target="tpu_custom_call" | custom-call | tf_op jit(solution)/shard_map/prepare/pallas_call | solution.py:436
  2.8 6.2 %collective-permute-start = (bf16[176,256]{1,0:T(8,128)(2,1)}, bf16[176,256]{1,0:T(8,128)(2,1)S(1)}, u32[]{:S(2)}, u32[]{:S(2)}) collective-permute-start(bf16[176,256]{1,0:T(8,128)(2,1)} %get-tuple-element.52), channel_id=1, source_target_pairs={{0,0},{1,8},{4,4},{5,12},{8,1},{9,9},{12,5},{13,13},{2,2},{3,10},{... | collective-permute-start | bytes 270344 | tf_op jit(solution)/shard_map/ppermute | solution.py:458
  9.0 0.6 collective-permute-start.1
  9.6 1.4 %collective-permute-done.2 = f32[8,128]{1,0:T(8,128)S(1)} collective-permute-done((f32[8,128]{1,0:T(8,128)}, f32[8,128]{1,0:T(8,128)S(1)}, u32[]{:S(2)}, u32[]{:S(2)}) %collective-permute-start.2) | collective-permute-done | bytes 4128 | tf_op jit(solution)/shard_map/ppermute | solution.py:45
  11.0 0.7 add.12
  11.7 1.2 %collective-permute-start.3 = (f32[8,128]{1,0:T(8,128)S(1)}, f32[8,128]{1,0:T(8,128)S(1)}, u32[]{:S(2)}, u32[]{:S(2)}) collective-permute-start(f32[8,128]{1,0:T(8,128)S(1)} %add.12), channel_id=1, source_target_pairs={{0,2},{2,0},{1,3},{3,1},{4,6},{6,4},{5,7},{7,5},{8,10},{10,8},{9,1... | collective-permute-start | bytes 12296 | tf_op jit(solution)/shard_map/ppermute | solution.py:45
  12.9 1.2 %collective-permute-done.3 = f32[8,128]{1,0:T(8,128)S(1)} collective-permute-done((f32[8,128]{1,0:T(8,128)S(1)}, f32[8,128]{1,0:T(8,128)S(1)}, u32[]{:S(2)}, u32[]{:S(2)}) %collective-permute-start.3) | collective-permute-done | bytes 4128 | tf_op jit(solution)/shard_map/ppermute | solution.py:45
  14.2 0.3 collective-permute-done.1.second_ref
  14.5 2.8 %collective-permute-start.4 = (bf16[320,256]{1,0:T(8,128)(2,1)S(1)}, bf16[320,256]{1,0:T(8,128)(2,1)S(1)}, u32[]{:S(2)}, u32[]{:S(2)}) collective-permute-start(bf16[320,256]{1,0:T(8,128)(2,1)S(1)} %shard_map.84.own_ref.refs_2_), channel_id=1, source_target_pairs={{0,128},{16,144},{32,160},{48,176},{64,192},{80,208},{96,224},{112... | collective-permute-start | bytes 491528 | tf_op jit(solution)/shard_map/ppermute | solution.py:40
  17.4 3.5 %collective-permute-done.4.eight_ref.refs_3_ = bf16[320,256]{1,0:T(8,128)(2,1)S(1)} collective-permute-done((bf16[320,256]{1,0:T(8,128)(2,1)S(1)}, bf16[320,256]{1,0:T(8,128)(2,1)S(1)}, u32[]{:S(2)}, u32[]{:S(2)}) %collective-permute-start.4) | collective-permute-done | bytes 163872 | tf_op jit(solution)/shard_map/ppermute | solution.py:40
  20.9 0.1 shard_map.85
  20.9 1.7 %collective-permute-start.5 = (bf16[464,256]{1,0:T(8,128)(2,1)S(1)}, bf16[464,256]{1,0:T(8,128)(2,1)S(1)}, u32[]{:S(2)}, u32[]{:S(2)}) collective-permute-start(bf16[464,256]{1,0:T(8,128)(2,1)S(1)} %get-tuple-element.55.refs_1_), channel_id=1, source_target_pairs={{0,16},{16,32},{32,48},{48,64},{64,80},{80,96},{96,112},{112,128},... | collective-permute-start | bytes 712712 | tf_op jit(solution)/shard_map/ppermute | solution.py:40
  22.6 6.5 %collective-permute-start.6 = (bf16[320,256]{1,0:T(8,128)(2,1)S(1)}, bf16[320,256]{1,0:T(8,128)(2,1)S(1)}, u32[]{:S(2)}, u32[]{:S(2)}) collective-permute-start(bf16[320,256]{1,0:T(8,128)(2,1)S(1)} %get-tuple-element.56), channel_id=1, source_target_pairs={{0,240},{16,0},{32,16},{48,32},{64,48},{80,64},{96,80},{112,96},{1... | collective-permute-start | bytes 491528 | tf_op jit(solution)/shard_map/ppermute | solution.py:40
  29.2 5.5 %collective-permute-start.8 = (bf16[128,1024]{1,0:T(8,128)(2,1)S(1)}, bf16[128,1024]{1,0:T(8,128)(2,1)S(1)}, u32[]{:S(2)}, u32[]{:S(2)}) collective-permute-start(bf16[128,1024]{1,0:T(8,128)(2,1)S(1)} %get-tuple-element.101), channel_id=1, source_target_pairs={{0,0},{1,8},{4,4},{5,12},{8,1},{9,9},{12,5},{13,13},{2,2},{3,10},{... | collective-permute-start | bytes 786440 | tf_op jit(solution)/shard_map/ppermute | solution.py:460
  34.7 0.6 collective-permute-start.9
  35.3 0.0 collective-permute-start.7
  35.3 0.0 collective-permute-done.6.seven_ref.refs_1_.refs_3_
  35.3 0.0 collective-permute-done.5.one_ref.refs_0_.refs_2_.refs_1_
  35.4 0.6 collective-permute-start.12
  36.0 4.1 %collective-permute-start.11 = (bf16[320,256]{1,0:T(8,128)(2,1)S(1)}, bf16[320,256]{1,0:T(8,128)(2,1)S(1)}, u32[]{:S(2)}, u32[]{:S(2)}) collective-permute-start(bf16[320,256]{1,0:T(8,128)(2,1)S(1)} %collective-permute-done.6.seven_ref.refs_1_.refs_3_), channel_id=1, source_target_pairs={{0,240},{16,0},{32,16},{48,32},{64,48},{80,64},{96,80},{112,96},{1... | collective-permute-start | bytes 491528 | tf_op jit(solution)/shard_map/ppermute | solution.py:40
  40.1 0.0 collective-permute-done.8.refs_0_
  40.1 0.0 collective-permute-start.10
  40.1 1.8 %collective-permute-done.9.refs_1_ = bf16[128,1024]{1,0:T(8,128)(2,1)S(1)} collective-permute-done((bf16[128,1024]{1,0:T(8,128)(2,1)S(1)}, bf16[128,1024]{1,0:T(8,128)(2,1)S(1)}, u32[]{:S(2)}, u32[]{:S(2)}) %collective-permute-start.9) | collective-permute-done | bytes 262176 | tf_op jit(solution)/shard_map/ppermute | solution.py:460
  41.8 2.1 %attend.5 = (bf16[2048,128]{1,0:T(8,128)(2,1)S(1)}, f32[32,128]{1,0:T(8,128)S(1)}, f32[2048,128]{1,0:T(8,128)S(1)}, f32[2048,128]{1,0:T(8,128)S(1)}, f32[2048,128]{1,0:T(8,128)S(1)}) custom-call(bf16[128,1024]{1,0:T(8,128)(2,1)S(1)} %collective-permute-done.8.refs_0_, bf16[128,1024]{1,0:T(8,128)(2,1)S(1)} %collective-permute-done.9.refs_1_, ...), custom_call_target="tpu_custom_call" | custom-call | flops 536870912 | bytes 1048576 | tf_op jit(solution)/shard_map/attend/pallas_call | solution.py:418
  43.9 0.0 collective-permute-done.7.refs_2_
  43.9 2.2 %attend.6 = (bf16[2048,128]{1,0:T(8,128)(2,1)S(1)}, f32[32,128]{1,0:T(8,128)S(1)}, f32[2048,128]{1,0:T(8,128)S(1)}, f32[2048,128]{1,0:T(8,128)S(1)}, f32[2048,128]{1,0:T(8,128)S(1)}) custom-call(bf16[464,256]{1,0:T(8,128)(2,1)S(1)} %collective-permute-done.5.one_ref.refs_0_.refs_2_.ref, ...), custom_call_target="tpu_custom_call", output_to_operand_aliasing={{0}: (3, {}), {1}: (4, {}), {2}: (5, {}), {3}: (6, {}), {4}... | custom-call | flops 1073741824 | bytes 1048576 | tf_op jit(solution)/shard_map/attend/pallas_call | solution.py:418
  46.1 0.0 collective-permute-done.11.refs_1_.second_ref.refs_5_
  46.1 3.0 %collective-permute-done.10.refs_0_.first_ref.refs_4_ = bf16[320,256]{1,0:T(8,128)(2,1)S(1)} collective-permute-done((bf16[320,256]{1,0:T(8,128)(2,1)S(1)}, bf16[320,256]{1,0:T(8,128)(2,1)S(1)}, u32[]{:S(2)}, u32[]{:S(2)}) %collective-permute-start.10) | collective-permute-done | bytes 163872 | tf_op jit(solution)/shard_map/ppermute | solution.py:40
  49.1 0.0 collective-permute-start.13
  49.1 5.1 %collective-permute-start.14 = (bf16[320,256]{1,0:T(8,128)(2,1)S(1)}, bf16[320,256]{1,0:T(8,128)(2,1)S(1)}, u32[]{:S(2)}, u32[]{:S(2)}) collective-permute-start(bf16[320,256]{1,0:T(8,128)(2,1)S(1)} %collective-permute-done.11.refs_1_.second_ref.refs_5_), channel_id=1, source_target_pairs={{0,240},{16,0},{32,16},{48,32},{64,48},{80,64},{96,80},{112,96},{1... | collective-permute-start | bytes 491528 | tf_op jit(solution)/shard_map/ppermute | solution.py:40
  54.2 1.9 %collective-permute-start.15 = (bf16[576,256]{1,0:T(8,128)(2,1)S(1)}, bf16[576,256]{1,0:T(8,128)(2,1)S(1)}, u32[]{:S(2)}, u32[]{:S(2)}) collective-permute-start(bf16[576,256]{1,0:T(8,128)(2,1)S(1)} %shard_map.87), channel_id=1, source_target_pairs={{0,1},{1,0},{2,3},{3,2},{4,5},{5,4},{6,7},{7,6},{8,9},{9,8},{10,11... | collective-permute-start | bytes 884744 | tf_op jit(solution)/shard_map/ppermute | solution.py:465
  56.0 0.0 collective-permute-done.12.refs_2_
  56.0 0.2 attend.7
  56.2 1.0 %collective-permute-done.13.refs_0_.refs_6_.first_ref = bf16[320,256]{1,0:T(8,128)(2,1)S(1)} collective-permute-done((bf16[320,256]{1,0:T(8,128)(2,1)S(1)}, bf16[320,256]{1,0:T(8,128)(2,1)S(1)}, u32[]{:S(2)}, u32[]{:S(2)}) %collective-permute-start.13) | collective-permute-done | bytes 163872 | tf_op jit(solution)/shard_map/ppermute | solution.py:40
  57.2 2.2 %collective-permute-start.18 = (bf16[576,256]{1,0:T(8,128)(2,1)S(1)}, bf16[576,256]{1,0:T(8,128)(2,1)S(1)}, u32[]{:S(2)}, u32[]{:S(2)}) collective-permute-start(bf16[576,256]{1,0:T(8,128)(2,1)S(1)} %shard_map.89), channel_id=1, source_target_pairs={{0,1},{1,0},{2,3},{3,2},{4,5},{5,4},{6,7},{7,6},{8,9},{9,8},{10,11... | collective-permute-start | bytes 884744 | tf_op jit(solution)/shard_map/ppermute | solution.py:465
  59.4 0.4 attend.8
  59.8 9.3 %collective-permute-done.16.refs_0_ = bf16[320,256]{1,0:T(8,128)(2,1)S(1)} collective-permute-done((bf16[320,256]{1,0:T(8,128)(2,1)S(1)}, bf16[320,256]{1,0:T(8,128)(2,1)S(1)}, u32[]{:S(2)}, u32[]{:S(2)}) %collective-permute-start.16) | collective-permute-done | bytes 163872 | tf_op jit(solution)/shard_map/ppermute | solution.py:40
  69.1 0.8 collective-permute-start.17
  70.0 1.6 %collective-permute-start.19 = (f32[32,128]{1,0:T(8,128)S(1)}, f32[32,128]{1,0:T(8,128)S(1)}, u32[]{:S(2)}, u32[]{:S(2)}) collective-permute-start(f32[32,128]{1,0:T(8,128)S(1)} %get-tuple-element.95), channel_id=1, source_target_pairs={{0,8},{4,12},{8,0},{12,4},{1,9},{5,13},{9,1},{13,5},{2,10},{6,14},... | collective-permute-start | bytes 49160 | tf_op jit(solution)/shard_map/ppermute | solution.py:540
  71.6 0.2 attend.9
  71.8 2.3 %collective-permute-done.19.refs_7_ = f32[32,128]{1,0:T(8,128)S(1)} collective-permute-done((f32[32,128]{1,0:T(8,128)S(1)}, f32[32,128]{1,0:T(8,128)S(1)}, u32[]{:S(2)}, u32[]{:S(2)}) %collective-permute-start.19) | collective-permute-done | bytes 16416 | tf_op jit(solution)/shard_map/ppermute | solution.py:540
  74.1 0.4 attend_last.2
  74.4 4.7 %collective-permute-start.20 = (bf16[144,1024]{1,0:T(8,128)(2,1)S(1)}, bf16[144,1024]{1,0:T(8,128)(2,1)S(1)}, u32[]{:S(2)}, u32[]{:S(2)}) collective-permute-start(bf16[144,1024]{1,0:T(8,128)(2,1)S(1)} %attend_last.2), channel_id=1, source_target_pairs={{0,0},{8,1},{4,4},{12,5},{1,8},{9,9},{5,12},{13,13},{2,2},{10,3},{... | collective-permute-start | bytes 884744 | tf_op jit(solution)/shard_map/ppermute | solution.py:560
  79.1 0.4 attend_last.3
  79.5 0.9 collective-permute-start.21
  80.4 6.2 %collective-permute-done.20.first_ref = bf16[144,1024]{1,0:T(8,128)(2,1)S(1)} collective-permute-done((bf16[144,1024]{1,0:T(8,128)(2,1)S(1)}, bf16[144,1024]{1,0:T(8,128)(2,1)S(1)}, u32[]{:S(2)}, u32[]{:S(2)}) %collective-permute-start.20) | collective-permute-done | bytes 294944 | tf_op jit(solution)/shard_map/ppermute | solution.py:560
  86.5 2.1 %collective-permute-done.21.second_ref = bf16[144,1024]{1,0:T(8,128)(2,1)S(1)} collective-permute-done((bf16[144,1024]{1,0:T(8,128)(2,1)S(1)}, bf16[144,1024]{1,0:T(8,128)(2,1)S(1)}, u32[]{:S(2)}, u32[]{:S(2)}) %collective-permute-start.21) | collective-permute-done | bytes 294944 | tf_op jit(solution)/shard_map/ppermute | solution.py:560
  88.6 0.8 shard_map.90
  (16 shorter events, 0.2 us)
Async XLA Ops:
  0.6 28.5 %copy-start = (bf16[128,2048]{1,0:T(8,128)(2,1)S(1)}, bf16[128,2048]{1,0:T(8,128)(2,1)}, u32[]{:S(2)}) copy-start(bf16[128,2048]{1,0:T(8,128)(2,1)} %param.5) | copy-start | bytes 1572868
  2.8 11.3 %collective-permute-start = (bf16[176,256]{1,0:T(8,128)(2,1)}, bf16[176,256]{1,0:T(8,128)(2,1)S(1)}, u32[]{:S(2)}, u32[]{:S(2)}) collective-permute-start(bf16[176,256]{1,0:T(8,128)(2,1)} %get-tuple-element.52), channel_id=1, source_target_pairs={{0,0},{1,8},{4,4},{5,12},{8,1},{9,9},{12,5},{13,13},{2,2},{3,10},{... | collective-permute-start | bytes 270344 | tf_op jit(solution)/shard_map/ppermute | solution.py:458
  9.0 5.5 %collective-permute-start.1 = (bf16[176,256]{1,0:T(8,128)(2,1)}, bf16[176,256]{1,0:T(8,128)(2,1)S(1)}, u32[]{:S(2)}, u32[]{:S(2)}) collective-permute-start(bf16[176,256]{1,0:T(8,128)(2,1)} %get-tuple-element.53), channel_id=1, source_target_pairs={{0,4},{1,12},{4,0},{5,8},{8,5},{9,13},{12,1},{13,9},{2,6},{3,14},{... | collective-permute-start | bytes 270344 | tf_op jit(solution)/shard_map/ppermute | solution.py:458
  9.6 1.4 %collective-permute-start.2 = (f32[8,128]{1,0:T(8,128)}, f32[8,128]{1,0:T(8,128)S(1)}, u32[]{:S(2)}, u32[]{:S(2)}) collective-permute-start(f32[8,128]{1,0:T(8,128)} %get-tuple-element.54), channel_id=1, source_target_pairs={{0,1},{1,0},{2,3},{3,2},{4,5},{5,4},{6,7},{7,6},{8,9},{9,8},{10,11... | collective-permute-start | bytes 12296 | tf_op jit(solution)/shard_map/ppermute | solution.py:45
  11.7 2.5 %collective-permute-start.3 = (f32[8,128]{1,0:T(8,128)S(1)}, f32[8,128]{1,0:T(8,128)S(1)}, u32[]{:S(2)}, u32[]{:S(2)}) collective-permute-start(f32[8,128]{1,0:T(8,128)S(1)} %add.12), channel_id=1, source_target_pairs={{0,2},{2,0},{1,3},{3,1},{4,6},{6,4},{5,7},{7,5},{8,10},{10,8},{9,1... | collective-permute-start | bytes 12296 | tf_op jit(solution)/shard_map/ppermute | solution.py:45
  14.5 6.4 %collective-permute-start.4 = (bf16[320,256]{1,0:T(8,128)(2,1)S(1)}, bf16[320,256]{1,0:T(8,128)(2,1)S(1)}, u32[]{:S(2)}, u32[]{:S(2)}) collective-permute-start(bf16[320,256]{1,0:T(8,128)(2,1)S(1)} %shard_map.84.own_ref.refs_2_), channel_id=1, source_target_pairs={{0,128},{16,144},{32,160},{48,176},{64,192},{80,208},{96,224},{112... | collective-permute-start | bytes 491528 | tf_op jit(solution)/shard_map/ppermute | solution.py:40
  20.9 14.4 %collective-permute-start.5 = (bf16[464,256]{1,0:T(8,128)(2,1)S(1)}, bf16[464,256]{1,0:T(8,128)(2,1)S(1)}, u32[]{:S(2)}, u32[]{:S(2)}) collective-permute-start(bf16[464,256]{1,0:T(8,128)(2,1)S(1)} %get-tuple-element.55.refs_1_), channel_id=1, source_target_pairs={{0,16},{16,32},{32,48},{48,64},{64,80},{80,96},{96,112},{112,128},... | collective-permute-start | bytes 712712 | tf_op jit(solution)/shard_map/ppermute | solution.py:40
  22.6 12.7 %collective-permute-start.6 = (bf16[320,256]{1,0:T(8,128)(2,1)S(1)}, bf16[320,256]{1,0:T(8,128)(2,1)S(1)}, u32[]{:S(2)}, u32[]{:S(2)}) collective-permute-start(bf16[320,256]{1,0:T(8,128)(2,1)S(1)} %get-tuple-element.56), channel_id=1, source_target_pairs={{0,240},{16,0},{32,16},{48,32},{64,48},{80,64},{96,80},{112,96},{1... | collective-permute-start | bytes 491528 | tf_op jit(solution)/shard_map/ppermute | solution.py:40
  29.2 10.9 %collective-permute-start.8 = (bf16[128,1024]{1,0:T(8,128)(2,1)S(1)}, bf16[128,1024]{1,0:T(8,128)(2,1)S(1)}, u32[]{:S(2)}, u32[]{:S(2)}) collective-permute-start(bf16[128,1024]{1,0:T(8,128)(2,1)S(1)} %get-tuple-element.101), channel_id=1, source_target_pairs={{0,0},{1,8},{4,4},{5,12},{8,1},{9,9},{12,5},{13,13},{2,2},{3,10},{... | collective-permute-start | bytes 786440 | tf_op jit(solution)/shard_map/ppermute | solution.py:460
  34.7 7.1 %collective-permute-start.9 = (bf16[128,1024]{1,0:T(8,128)(2,1)S(1)}, bf16[128,1024]{1,0:T(8,128)(2,1)S(1)}, u32[]{:S(2)}, u32[]{:S(2)}) collective-permute-start(bf16[128,1024]{1,0:T(8,128)(2,1)S(1)} %get-tuple-element.100), channel_id=1, source_target_pairs={{0,4},{1,12},{4,0},{5,8},{8,5},{9,13},{12,1},{13,9},{2,6},{3,14},{... | collective-permute-start | bytes 786440 | tf_op jit(solution)/shard_map/ppermute | solution.py:460
  35.3 8.6 %collective-permute-start.7 = (bf16[576,256]{1,0:T(8,128)(2,1)S(1)}, bf16[576,256]{1,0:T(8,128)(2,1)S(1)}, u32[]{:S(2)}, u32[]{:S(2)}) collective-permute-start(bf16[576,256]{1,0:T(8,128)(2,1)S(1)} %get-tuple-element.57), channel_id=1, source_target_pairs={{0,1},{1,0},{2,3},{3,2},{4,5},{5,4},{6,7},{7,6},{8,9},{9,8},{10,11... | collective-permute-start | bytes 884744 | tf_op jit(solution)/shard_map/ppermute | solution.py:465
  35.4 20.7 %collective-permute-start.12 = (bf16[720,256]{1,0:T(8,128)(2,1)S(1)}, bf16[720,256]{1,0:T(8,128)(2,1)S(1)}, u32[]{:S(2)}, u32[]{:S(2)}) collective-permute-start(bf16[720,256]{1,0:T(8,128)(2,1)S(1)} %get-tuple-element.68), channel_id=1, source_target_pairs={{0,1},{1,0},{2,3},{3,2},{4,5},{5,4},{6,7},{7,6},{8,9},{9,8},{10,11... | collective-permute-start | bytes 1105928 | tf_op jit(solution)/shard_map/ppermute | solution.py:465
  36.0 10.1 %collective-permute-start.11 = (bf16[320,256]{1,0:T(8,128)(2,1)S(1)}, bf16[320,256]{1,0:T(8,128)(2,1)S(1)}, u32[]{:S(2)}, u32[]{:S(2)}) collective-permute-start(bf16[320,256]{1,0:T(8,128)(2,1)S(1)} %collective-permute-done.6.seven_ref.refs_1_.refs_3_), channel_id=1, source_target_pairs={{0,240},{16,0},{32,16},{48,32},{64,48},{80,64},{96,80},{112,96},{1... | collective-permute-start | bytes 491528 | tf_op jit(solution)/shard_map/ppermute | solution.py:40
  40.1 9.0 %collective-permute-start.10 = (bf16[320,256]{1,0:T(8,128)(2,1)S(1)}, bf16[320,256]{1,0:T(8,128)(2,1)S(1)}, u32[]{:S(2)}, u32[]{:S(2)}) collective-permute-start(bf16[320,256]{1,0:T(8,128)(2,1)S(1)} %get-tuple-element.58), channel_id=1, source_target_pairs={{0,16},{16,32},{32,48},{48,64},{64,80},{80,96},{96,112},{112,128},... | collective-permute-start | bytes 491528 | tf_op jit(solution)/shard_map/ppermute | solution.py:40
  49.1 8.1 %collective-permute-start.13 = (bf16[320,256]{1,0:T(8,128)(2,1)S(1)}, bf16[320,256]{1,0:T(8,128)(2,1)S(1)}, u32[]{:S(2)}, u32[]{:S(2)}) collective-permute-start(bf16[320,256]{1,0:T(8,128)(2,1)S(1)} %collective-permute-done.10.refs_0_.first_ref.refs_4_), channel_id=1, source_target_pairs={{0,16},{16,32},{32,48},{48,64},{64,80},{80,96},{96,112},{112,128},... | collective-permute-start | bytes 491528 | tf_op jit(solution)/shard_map/ppermute | solution.py:40
  49.1 8.1 %collective-permute-start.14 = (bf16[320,256]{1,0:T(8,128)(2,1)S(1)}, bf16[320,256]{1,0:T(8,128)(2,1)S(1)}, u32[]{:S(2)}, u32[]{:S(2)}) collective-permute-start(bf16[320,256]{1,0:T(8,128)(2,1)S(1)} %collective-permute-done.11.refs_1_.second_ref.refs_5_), channel_id=1, source_target_pairs={{0,240},{16,0},{32,16},{48,32},{64,48},{80,64},{96,80},{112,96},{1... | collective-permute-start | bytes 491528 | tf_op jit(solution)/shard_map/ppermute | solution.py:40
  54.2 5.2 %collective-permute-start.15 = (bf16[576,256]{1,0:T(8,128)(2,1)S(1)}, bf16[576,256]{1,0:T(8,128)(2,1)S(1)}, u32[]{:S(2)}, u32[]{:S(2)}) collective-permute-start(bf16[576,256]{1,0:T(8,128)(2,1)S(1)} %shard_map.87), channel_id=1, source_target_pairs={{0,1},{1,0},{2,3},{3,2},{4,5},{5,4},{6,7},{7,6},{8,9},{9,8},{10,11... | collective-permute-start | bytes 884744 | tf_op jit(solution)/shard_map/ppermute | solution.py:465
  57.2 14.4 %collective-permute-start.18 = (bf16[576,256]{1,0:T(8,128)(2,1)S(1)}, bf16[576,256]{1,0:T(8,128)(2,1)S(1)}, u32[]{:S(2)}, u32[]{:S(2)}) collective-permute-start(bf16[576,256]{1,0:T(8,128)(2,1)S(1)} %shard_map.89), channel_id=1, source_target_pairs={{0,1},{1,0},{2,3},{3,2},{4,5},{5,4},{6,7},{7,6},{8,9},{9,8},{10,11... | collective-permute-start | bytes 884744 | tf_op jit(solution)/shard_map/ppermute | solution.py:465
  59.4 9.7 %collective-permute-start.16 = (bf16[320,256]{1,0:T(8,128)(2,1)S(1)}, bf16[320,256]{1,0:T(8,128)(2,1)S(1)}, u32[]{:S(2)}, u32[]{:S(2)}) collective-permute-start(bf16[320,256]{1,0:T(8,128)(2,1)S(1)} %collective-permute-done.13.refs_0_.refs_6_.first_ref), channel_id=1, source_target_pairs={{0,16},{16,32},{32,48},{48,64},{64,80},{80,96},{96,112},{112,128},... | collective-permute-start | bytes 491528 | tf_op jit(solution)/shard_map/ppermute | solution.py:40
  69.1 4.9 %collective-permute-start.17 = (bf16[320,256]{1,0:T(8,128)(2,1)S(1)}, bf16[320,256]{1,0:T(8,128)(2,1)S(1)}, u32[]{:S(2)}, u32[]{:S(2)}) collective-permute-start(bf16[320,256]{1,0:T(8,128)(2,1)S(1)} %get-tuple-element.84.refs_0_.refs_1_), channel_id=1, source_target_pairs={{0,1},{1,0},{2,3},{3,2},{4,5},{5,4},{6,7},{7,6},{8,9},{9,8},{10,11... | collective-permute-start | bytes 491528 | tf_op jit(solution)/shard_map/ppermute | solution.py:465
  70.0 4.1 %collective-permute-start.19 = (f32[32,128]{1,0:T(8,128)S(1)}, f32[32,128]{1,0:T(8,128)S(1)}, u32[]{:S(2)}, u32[]{:S(2)}) collective-permute-start(f32[32,128]{1,0:T(8,128)S(1)} %get-tuple-element.95), channel_id=1, source_target_pairs={{0,8},{4,12},{8,0},{12,4},{1,9},{5,13},{9,1},{13,5},{2,10},{6,14},... | collective-permute-start | bytes 49160 | tf_op jit(solution)/shard_map/ppermute | solution.py:540
  74.4 12.1 %collective-permute-start.20 = (bf16[144,1024]{1,0:T(8,128)(2,1)S(1)}, bf16[144,1024]{1,0:T(8,128)(2,1)S(1)}, u32[]{:S(2)}, u32[]{:S(2)}) collective-permute-start(bf16[144,1024]{1,0:T(8,128)(2,1)S(1)} %attend_last.2), channel_id=1, source_target_pairs={{0,0},{8,1},{4,4},{12,5},{1,8},{9,9},{5,12},{13,13},{2,2},{10,3},{... | collective-permute-start | bytes 884744 | tf_op jit(solution)/shard_map/ppermute | solution.py:560
  79.5 9.1 %collective-permute-start.21 = (bf16[144,1024]{1,0:T(8,128)(2,1)S(1)}, bf16[144,1024]{1,0:T(8,128)(2,1)S(1)}, u32[]{:S(2)}, u32[]{:S(2)}) collective-permute-start(bf16[144,1024]{1,0:T(8,128)(2,1)S(1)} %attend_last.3), channel_id=1, source_target_pairs={{4,0},{12,1},{0,4},{8,5},{5,8},{13,9},{1,12},{9,13},{6,2},{14,3},{... | collective-permute-start | bytes 884744 | tf_op jit(solution)/shard_map/ppermute | solution.py:560

commit v2 on v1

--- a/solution.py
+++ b/solution.py
@@ -508,20 +508,13 @@
         ),
         state,
     )
+    state = attend(None, [other_two_six], ((piece(0, 0, 2, True), piece(0, HALF, 6, True)),), state)
 
     three, five = after(state, three, five)
     four = shifted(three, 1)
     (both,) = small(pair_kernel, [rows(2 * HALF)], three, five)
     other_three_five = partner(both)
-    state = attend(
-        None,
-        [three, five, other_two_six],
-        (
-            (piece(0, 0, 3, False), piece(1, 0, 5, False)),
-            (piece(2, 0, 2, True), piece(2, HALF, 6, True)),
-        ),
-        state,
-    )
+    state = attend(None, [three, five], ((piece(0, 0, 3, False), piece(1, 0, 5, False)),), state)
 
     (four,) = after(state, four)
     four, energy = small(
@@ -539,23 +532,21 @@
     other_four = partner(four)
     energy = lax.ppermute(energy, "y", [(i, i ^ 2) for i in range(4)])
     state = attend(
-        None,
-        [four, one, other_one_seven, other_three_five],
+        None, [other_three_five], ((piece(0, 0, 3, True), piece(0, HALF, 5, True)),), state
+    )
+    units = (
         (
-            (
-                piece(0, 0, 4, False),
-                piece(1, HALF + RIDER, 9, False),
-                piece(2, 2 * HALF, 9, True),
-            ),
-            (piece(3, 0, 3, True), piece(3, HALF, 5, True)),
+            piece(1, 0, 4, False),
+            piece(2, HALF + RIDER, 9, False),
+            piece(3, 2 * HALF, 9, True),
         ),
-        state,
-    )
-    units = ((piece(0, 0, 4, True),),)
+        (piece(0, 0, 4, True),),
+    )
+    arrays = [other_four, four, one, other_one_seven]
     back = []
     for t in range(2):
         (mixed,) = attend(
-            None, [other_four, four], units, state, t, HALF, energy
+            None, arrays, units, state, t, HALF, energy
         )
         back.append(lax.ppermute(mixed, COLUMN, [(d, s) for s, d in to_heads(t)]))
     attention, captured, share = small(

time: 89.7 us -> 93.3 us (1.040); the launches traced: 89.5 us -> 91.9 us
  waiting for transfers between devices: 32 us -> 34.7 us
    ppermute x8, waiting for transfers between devices: 16.8 us -> 20.9 us  [shifted(): lax.ppermute(array, RING, [(i, (i + by) % SLABS) for i in range(SLABS)])]
    ppermute x2, waiting for transfers between devices: 1.77 us -> 0.01 us  [body(): q = [lax.ppermute(slices[t], COLUMN, to_heads(t)) for t in range(2)]]
    ppermute x8, starting transfers between devices: 20.2 us -> 21.3 us  [shifted(): lax.ppermute(array, RING, [(i, (i + by) % SLABS) for i in range(SLABS)])]
    pallas_call x7 -> x8, Pallas kernels: 5.75 us -> 5.89 us  [attend(): pl.pallas_call(functools.partial(attend_kernel, len(arrays), units, tiles...]
  transfers between devices with their start and end apart: 22 -> 22, of which waited for: 11 -> 10; matrix products, arithmetic and copies ran while one was open for 1% -> 1% of each run, Pallas kernels for 6% -> 6%
where the time goes in v2:
time: 93.3 us; the launch traced here: 91.9 us
  starting transfers between devices  46.5 us (50%)
  waiting for transfers between devices  34.7 us (37%)
  Pallas kernels  9.09 us (10%)
    ppermute x8, starting transfers between devices, shifted(): lax.ppermute(array, RING, [(i, (i + by) % SLABS) for i in range(SLABS)])  21.3 us
    ppermute x8, waiting for transfers between devices, shifted(): lax.ppermute(array, RING, [(i, (i + by) % SLABS) for i in range(SLABS)])  20.9 us
    ppermute x2, waiting for transfers between devices, body(): back.append(lax.ppermute(mixed, COLUMN, [(d, s) for s, d in to_heads(t)]))  8.55 us
    ppermute x2, starting transfers between devices, body(): kv.append(lax.ppermute(array, COLUMN, to_heads(t)))  6.8 us
    pallas_call x8, Pallas kernels, attend(): pl.pallas_call(functools.partial(attend_kernel, len(arrays), units, tiles...  5.89 us
    ppermute x2, starting transfers between devices, body(): q = [lax.ppermute(slices[t], COLUMN, to_heads(t)) for t in range(2)]  5.56 us
    ppermute x2, starting transfers between devices, body(): back.append(lax.ppermute(mixed, COLUMN, [(d, s) for s, d in to_heads(t)]))  5.24 us
    ppermute x5, starting transfers between devices, partner(): return lax.ppermute(array, 'c', [(0, 1), (1, 0)])  4.83 us
  transfers between devices with their start and end apart: 22, of which 10 were waited for; matrix products, arithmetic and copies ran while one was open for 1% of the time, Pallas kernels for 6%

profile of v2, /device:TPU:1, one launch (start us, length us, event | category | flops | bytes accessed | tf_op | source)
XLA Modules:
  0.0 91.9 jit_solution(16255432816272223447)
XLA Ops:
  0.6 2.2 %prepare.1 = (bf16[176,256]{1,0:T(8,128)(2,1)}, bf16[176,256]{1,0:T(8,128)(2,1)}, bf16[128,128]{1,0:T(8,128)(2,1)}, f32[8,128]{1,0:T(8,128)}) custom-call(bf16[128,256]{1,0:T(8,128)(2,1)} %keys_hbm.1, bf16[128,256]{1,0:T(8,128)(2,1)} %values_hbm.1, s32[1,128]{1,0:T(1,128)} %bitcast.4, bf16[2,2,32,128]{3,2,1,0:T(8,128)(2,1)} %bitcast.3), custom_call_target="tpu_custom_call" | custom-call | tf_op jit(solution)/shard_map/prepare/pallas_call | solution.py:436
  2.8 6.2 %collective-permute-start = (bf16[176,256]{1,0:T(8,128)(2,1)}, bf16[176,256]{1,0:T(8,128)(2,1)S(1)}, u32[]{:S(2)}, u32[]{:S(2)}) collective-permute-start(bf16[176,256]{1,0:T(8,128)(2,1)} %get-tuple-element.57), channel_id=1, source_target_pairs={{0,0},{1,8},{4,4},{5,12},{8,1},{9,9},{12,5},{13,13},{2,2},{3,10},{... | collective-permute-start | bytes 270344 | tf_op jit(solution)/shard_map/ppermute | solution.py:458
  9.0 0.6 collective-permute-start.1
  9.6 1.4 %collective-permute-done.2 = f32[8,128]{1,0:T(8,128)S(1)} collective-permute-done((f32[8,128]{1,0:T(8,128)}, f32[8,128]{1,0:T(8,128)S(1)}, u32[]{:S(2)}, u32[]{:S(2)}) %collective-permute-start.2) | collective-permute-done | bytes 4128 | tf_op jit(solution)/shard_map/ppermute | solution.py:45
  11.0 0.7 add.12
  11.7 1.2 %collective-permute-start.3 = (f32[8,128]{1,0:T(8,128)S(1)}, f32[8,128]{1,0:T(8,128)S(1)}, u32[]{:S(2)}, u32[]{:S(2)}) collective-permute-start(f32[8,128]{1,0:T(8,128)S(1)} %add.12), channel_id=1, source_target_pairs={{0,2},{2,0},{1,3},{3,1},{4,6},{6,4},{5,7},{7,5},{8,10},{10,8},{9,1... | collective-permute-start | bytes 12296 | tf_op jit(solution)/shard_map/ppermute | solution.py:45
  12.9 1.2 %collective-permute-done.3 = f32[8,128]{1,0:T(8,128)S(1)} collective-permute-done((f32[8,128]{1,0:T(8,128)S(1)}, f32[8,128]{1,0:T(8,128)S(1)}, u32[]{:S(2)}, u32[]{:S(2)}) %collective-permute-start.3) | collective-permute-done | bytes 4128 | tf_op jit(solution)/shard_map/ppermute | solution.py:45
  14.2 0.3 collective-permute-done.1.second_ref
  14.5 2.8 %collective-permute-start.4 = (bf16[320,256]{1,0:T(8,128)(2,1)S(1)}, bf16[320,256]{1,0:T(8,128)(2,1)S(1)}, u32[]{:S(2)}, u32[]{:S(2)}) collective-permute-start(bf16[320,256]{1,0:T(8,128)(2,1)S(1)} %shard_map.84.own_ref.refs_2_), channel_id=1, source_target_pairs={{0,128},{16,144},{32,160},{48,176},{64,192},{80,208},{96,224},{112... | collective-permute-start | bytes 491528 | tf_op jit(solution)/shard_map/ppermute | solution.py:40
  17.4 5.0 %collective-permute-start.8 = (bf16[128,1024]{1,0:T(8,128)(2,1)S(1)}, bf16[128,1024]{1,0:T(8,128)(2,1)S(1)}, u32[]{:S(2)}, u32[]{:S(2)}) collective-permute-start(bf16[128,1024]{1,0:T(8,128)(2,1)S(1)} %get-tuple-element.111), channel_id=1, source_target_pairs={{0,0},{1,8},{4,4},{5,12},{8,1},{9,9},{12,5},{13,13},{2,2},{3,10},{... | collective-permute-start | bytes 786440 | tf_op jit(solution)/shard_map/ppermute | solution.py:460
  22.4 0.6 collective-permute-start.9
  23.0 0.1 shard_map.85
  23.0 1.7 %collective-permute-start.5 = (bf16[464,256]{1,0:T(8,128)(2,1)S(1)}, bf16[464,256]{1,0:T(8,128)(2,1)S(1)}, u32[]{:S(2)}, u32[]{:S(2)}) collective-permute-start(bf16[464,256]{1,0:T(8,128)(2,1)S(1)} %get-tuple-element.60.refs_1_), channel_id=1, source_target_pairs={{0,16},{16,32},{32,48},{48,64},{64,80},{80,96},{96,112},{112,128},... | collective-permute-start | bytes 712712 | tf_op jit(solution)/shard_map/ppermute | solution.py:40
  24.7 0.0 collective-permute-start.7
  24.8 6.2 %collective-permute-start.6 = (bf16[320,256]{1,0:T(8,128)(2,1)S(1)}, bf16[320,256]{1,0:T(8,128)(2,1)S(1)}, u32[]{:S(2)}, u32[]{:S(2)}) collective-permute-start(bf16[320,256]{1,0:T(8,128)(2,1)S(1)} %get-tuple-element.61), channel_id=1, source_target_pairs={{0,240},{16,0},{32,16},{48,32},{64,48},{80,64},{96,80},{112,96},{1... | collective-permute-start | bytes 491528 | tf_op jit(solution)/shard_map/ppermute | solution.py:40
  31.0 3.5 %collective-permute-done.6.seven_ref.refs_1_.refs_3_ = bf16[320,256]{1,0:T(8,128)(2,1)S(1)} collective-permute-done((bf16[320,256]{1,0:T(8,128)(2,1)S(1)}, bf16[320,256]{1,0:T(8,128)(2,1)S(1)}, u32[]{:S(2)}, u32[]{:S(2)}) %collective-permute-start.6) | collective-permute-done | bytes 163872 | tf_op jit(solution)/shard_map/ppermute | solution.py:40
  34.5 0.0 collective-permute-done.5.one_ref.refs_0_.refs_2_
  34.5 1.4 %collective-permute-start.13 = (bf16[720,256]{1,0:T(8,128)(2,1)S(1)}, bf16[720,256]{1,0:T(8,128)(2,1)S(1)}, u32[]{:S(2)}, u32[]{:S(2)}) collective-permute-start(bf16[720,256]{1,0:T(8,128)(2,1)S(1)} %get-tuple-element.73), channel_id=1, source_target_pairs={{0,1},{1,0},{2,3},{3,2},{4,5},{5,4},{6,7},{7,6},{8,9},{9,8},{10,11... | collective-permute-start | bytes 1105928 | tf_op jit(solution)/shard_map/ppermute | solution.py:465
  35.9 5.4 %collective-permute-start.11 = (bf16[320,256]{1,0:T(8,128)(2,1)S(1)}, bf16[320,256]{1,0:T(8,128)(2,1)S(1)}, u32[]{:S(2)}, u32[]{:S(2)}) collective-permute-start(bf16[320,256]{1,0:T(8,128)(2,1)S(1)} %collective-permute-done.6.seven_ref.refs_1_.refs_3_), channel_id=1, source_target_pairs={{0,240},{16,0},{32,16},{48,32},{64,48},{80,64},{96,80},{112,96},{1... | collective-permute-start | bytes 491528 | tf_op jit(solution)/shard_map/ppermute | solution.py:40
  41.4 0.0 collective-permute-done.8.refs_0_
  41.4 2.1 %attend.6 = (bf16[2048,128]{1,0:T(8,128)(2,1)S(1)}, f32[32,128]{1,0:T(8,128)S(1)}, f32[2048,128]{1,0:T(8,128)S(1)}, f32[2048,128]{1,0:T(8,128)S(1)}, f32[2048,128]{1,0:T(8,128)S(1)}) custom-call(bf16[128,1024]{1,0:T(8,128)(2,1)S(1)} %collective-permute-done.8.refs_0_, bf16[128,1024]{1,0:T(8,128)(2,1)S(1)} %collective-permute-done.9.refs_1_, ...), custom_call_target="tpu_custom_call" | custom-call | flops 536870912 | bytes 1048576 | tf_op jit(solution)/shard_map/attend/pallas_call | solution.py:418
  43.4 0.0 collective-permute-done.7.refs_2_
  43.5 2.1 %attend.7 = (bf16[2048,128]{1,0:T(8,128)(2,1)S(1)}, f32[32,128]{1,0:T(8,128)S(1)}, f32[2048,128]{1,0:T(8,128)S(1)}, f32[2048,128]{1,0:T(8,128)S(1)}, f32[2048,128]{1,0:T(8,128)S(1)}) custom-call(bf16[464,256]{1,0:T(8,128)(2,1)S(1)} %collective-permute-done.5.one_ref.refs_0_.refs_2_, ...), custom_call_target="tpu_custom_call", output_to_operand_aliasing={{0}: (3, {}), {1}: (4, {}), {2}: (5, {}), {3}: (6, {}), {4}... | custom-call | flops 1073741824 | bytes 1048576 | tf_op jit(solution)/shard_map/attend/pallas_call | solution.py:418
  45.6 0.0 collective-permute-done.11.second_ref.refs_1_.refs_5_
  45.6 4.7 %collective-permute-done.10.first_ref.refs_0_.refs_4_ = bf16[320,256]{1,0:T(8,128)(2,1)S(1)} collective-permute-done((bf16[320,256]{1,0:T(8,128)(2,1)S(1)}, bf16[320,256]{1,0:T(8,128)(2,1)S(1)}, u32[]{:S(2)}, u32[]{:S(2)}) %collective-permute-start.10) | collective-permute-done | bytes 163872 | tf_op jit(solution)/shard_map/ppermute | solution.py:40
  50.4 1.3 %collective-permute-start.12 = (bf16[576,256]{1,0:T(8,128)(2,1)S(1)}, bf16[576,256]{1,0:T(8,128)(2,1)S(1)}, u32[]{:S(2)}, u32[]{:S(2)}) collective-permute-start(bf16[576,256]{1,0:T(8,128)(2,1)S(1)} %shard_map.87), channel_id=1, source_target_pairs={{0,1},{1,0},{2,3},{3,2},{4,5},{5,4},{6,7},{7,6},{8,9},{9,8},{10,11... | collective-permute-start | bytes 884744 | tf_op jit(solution)/shard_map/ppermute | solution.py:465
  51.7 0.0 collective-permute-start.14
  51.7 5.1 %collective-permute-start.15 = (bf16[320,256]{1,0:T(8,128)(2,1)S(1)}, bf16[320,256]{1,0:T(8,128)(2,1)S(1)}, u32[]{:S(2)}, u32[]{:S(2)}) collective-permute-start(bf16[320,256]{1,0:T(8,128)(2,1)S(1)} %collective-permute-done.11.second_ref.refs_1_.refs_5_), channel_id=1, source_target_pairs={{0,240},{16,0},{32,16},{48,32},{64,48},{80,64},{96,80},{112,96},{1... | collective-permute-start | bytes 491528 | tf_op jit(solution)/shard_map/ppermute | solution.py:40
  56.8 0.0 collective-permute-done.13.refs_2_.refs_3_
  56.8 0.2 attend.8
  57.0 0.0 collective-permute-done.12.refs_0_
  57.0 0.2 attend.9
  57.2 3.8 %collective-permute-done.14.refs_0_.refs_6_.first_ref = bf16[320,256]{1,0:T(8,128)(2,1)S(1)} collective-permute-done((bf16[320,256]{1,0:T(8,128)(2,1)S(1)}, bf16[320,256]{1,0:T(8,128)(2,1)S(1)}, u32[]{:S(2)}, u32[]{:S(2)}) %collective-permute-start.14) | collective-permute-done | bytes 163872 | tf_op jit(solution)/shard_map/ppermute | solution.py:40
  61.0 0.0 collective-permute-done.15.refs_1_.refs_7_.second_ref
  61.0 1.0 %collective-permute-start.18 = (bf16[576,256]{1,0:T(8,128)(2,1)S(1)}, bf16[576,256]{1,0:T(8,128)(2,1)S(1)}, u32[]{:S(2)}, u32[]{:S(2)}) collective-permute-start(bf16[576,256]{1,0:T(8,128)(2,1)S(1)} %shard_map.89), channel_id=1, source_target_pairs={{0,1},{1,0},{2,3},{3,2},{4,5},{5,4},{6,7},{7,6},{8,9},{9,8},{10,11... | collective-permute-start | bytes 884744 | tf_op jit(solution)/shard_map/ppermute | solution.py:465
  62.1 0.4 attend.10
  62.4 8.9 %collective-permute-done.16.refs_0_ = bf16[320,256]{1,0:T(8,128)(2,1)S(1)} collective-permute-done((bf16[320,256]{1,0:T(8,128)(2,1)S(1)}, bf16[320,256]{1,0:T(8,128)(2,1)S(1)}, u32[]{:S(2)}, u32[]{:S(2)}) %collective-permute-start.16) | collective-permute-done | bytes 163872 | tf_op jit(solution)/shard_map/ppermute | solution.py:40
  71.4 1.0 %collective-permute-start.17 = (bf16[320,256]{1,0:T(8,128)(2,1)S(1)}, bf16[320,256]{1,0:T(8,128)(2,1)S(1)}, u32[]{:S(2)}, u32[]{:S(2)}) collective-permute-start(bf16[320,256]{1,0:T(8,128)(2,1)S(1)} %get-tuple-element.94.refs_1_), channel_id=1, source_target_pairs={{0,1},{1,0},{2,3},{3,2},{4,5},{5,4},{6,7},{7,6},{8,9},{9,8},{10,11... | collective-permute-start | bytes 491528 | tf_op jit(solution)/shard_map/ppermute | solution.py:465
  72.4 1.6 %collective-permute-start.19 = (f32[32,128]{1,0:T(8,128)S(1)}, f32[32,128]{1,0:T(8,128)S(1)}, u32[]{:S(2)}, u32[]{:S(2)}) collective-permute-start(f32[32,128]{1,0:T(8,128)S(1)} %get-tuple-element.105), channel_id=1, source_target_pairs={{0,8},{4,12},{8,0},{12,4},{1,9},{5,13},{9,1},{13,5},{2,10},{6,14},... | collective-permute-start | bytes 49160 | tf_op jit(solution)/shard_map/ppermute | solution.py:533
  74.0 0.2 attend.11
  74.2 2.3 %collective-permute-done.19.refs_9_ = f32[32,128]{1,0:T(8,128)S(1)} collective-permute-done((f32[32,128]{1,0:T(8,128)S(1)}, f32[32,128]{1,0:T(8,128)S(1)}, u32[]{:S(2)}, u32[]{:S(2)}) %collective-permute-start.19) | collective-permute-done | bytes 16416 | tf_op jit(solution)/shard_map/ppermute | solution.py:533
  76.5 0.4 attend_last.2
  76.9 4.7 %collective-permute-start.20 = (bf16[144,1024]{1,0:T(8,128)(2,1)S(1)}, bf16[144,1024]{1,0:T(8,128)(2,1)S(1)}, u32[]{:S(2)}, u32[]{:S(2)}) collective-permute-start(bf16[144,1024]{1,0:T(8,128)(2,1)S(1)} %attend_last.2), channel_id=1, source_target_pairs={{0,0},{8,1},{4,4},{12,5},{1,8},{9,9},{5,12},{13,13},{2,2},{10,3},{... | collective-permute-start | bytes 884744 | tf_op jit(solution)/shard_map/ppermute | solution.py:551
  81.6 0.4 attend_last.3
  82.0 0.6 collective-permute-start.21
  82.5 6.2 %collective-permute-done.20.first_ref = bf16[144,1024]{1,0:T(8,128)(2,1)S(1)} collective-permute-done((bf16[144,1024]{1,0:T(8,128)(2,1)S(1)}, bf16[144,1024]{1,0:T(8,128)(2,1)S(1)}, u32[]{:S(2)}, u32[]{:S(2)}) %collective-permute-start.20) | collective-permute-done | bytes 294944 | tf_op jit(solution)/shard_map/ppermute | solution.py:551
  88.7 2.4 %collective-permute-done.21.second_ref = bf16[144,1024]{1,0:T(8,128)(2,1)S(1)} collective-permute-done((bf16[144,1024]{1,0:T(8,128)(2,1)S(1)}, bf16[144,1024]{1,0:T(8,128)(2,1)S(1)}, u32[]{:S(2)}, u32[]{:S(2)}) %collective-permute-start.21) | collective-permute-done | bytes 294944 | tf_op jit(solution)/shard_map/ppermute | solution.py:551
  91.1 0.8 shard_map.90
  (17 shorter events, 0.2 us)
Async XLA Ops:
  0.6 16.7 %copy-start = (bf16[128,2048]{1,0:T(8,128)(2,1)S(1)}, bf16[128,2048]{1,0:T(8,128)(2,1)}, u32[]{:S(2)}) copy-start(bf16[128,2048]{1,0:T(8,128)(2,1)} %param.5) | copy-start | bytes 1572868
  2.8 11.3 %collective-permute-start = (bf16[176,256]{1,0:T(8,128)(2,1)}, bf16[176,256]{1,0:T(8,128)(2,1)S(1)}, u32[]{:S(2)}, u32[]{:S(2)}) collective-permute-start(bf16[176,256]{1,0:T(8,128)(2,1)} %get-tuple-element.57), channel_id=1, source_target_pairs={{0,0},{1,8},{4,4},{5,12},{8,1},{9,9},{12,5},{13,13},{2,2},{3,10},{... | collective-permute-start | bytes 270344 | tf_op jit(solution)/shard_map/ppermute | solution.py:458
  9.0 5.5 %collective-permute-start.1 = (bf16[176,256]{1,0:T(8,128)(2,1)}, bf16[176,256]{1,0:T(8,128)(2,1)S(1)}, u32[]{:S(2)}, u32[]{:S(2)}) collective-permute-start(bf16[176,256]{1,0:T(8,128)(2,1)} %get-tuple-element.58), channel_id=1, source_target_pairs={{0,4},{1,12},{4,0},{5,8},{8,5},{9,13},{12,1},{13,9},{2,6},{3,14},{... | collective-permute-start | bytes 270344 | tf_op jit(solution)/shard_map/ppermute | solution.py:458
  9.6 1.4 %collective-permute-start.2 = (f32[8,128]{1,0:T(8,128)}, f32[8,128]{1,0:T(8,128)S(1)}, u32[]{:S(2)}, u32[]{:S(2)}) collective-permute-start(f32[8,128]{1,0:T(8,128)} %get-tuple-element.59), channel_id=1, source_target_pairs={{0,1},{1,0},{2,3},{3,2},{4,5},{5,4},{6,7},{7,6},{8,9},{9,8},{10,11... | collective-permute-start | bytes 12296 | tf_op jit(solution)/shard_map/ppermute | solution.py:45
  11.7 2.5 %collective-permute-start.3 = (f32[8,128]{1,0:T(8,128)S(1)}, f32[8,128]{1,0:T(8,128)S(1)}, u32[]{:S(2)}, u32[]{:S(2)}) collective-permute-start(f32[8,128]{1,0:T(8,128)S(1)} %add.12), channel_id=1, source_target_pairs={{0,2},{2,0},{1,3},{3,1},{4,6},{6,4},{5,7},{7,5},{8,10},{10,8},{9,1... | collective-permute-start | bytes 12296 | tf_op jit(solution)/shard_map/ppermute | solution.py:45
  14.5 8.4 %collective-permute-start.4 = (bf16[320,256]{1,0:T(8,128)(2,1)S(1)}, bf16[320,256]{1,0:T(8,128)(2,1)S(1)}, u32[]{:S(2)}, u32[]{:S(2)}) collective-permute-start(bf16[320,256]{1,0:T(8,128)(2,1)S(1)} %shard_map.84.own_ref.refs_2_), channel_id=1, source_target_pairs={{0,128},{16,144},{32,160},{48,176},{64,192},{80,208},{96,224},{112... | collective-permute-start | bytes 491528 | tf_op jit(solution)/shard_map/ppermute | solution.py:40
  17.4 24.0 %collective-permute-start.8 = (bf16[128,1024]{1,0:T(8,128)(2,1)S(1)}, bf16[128,1024]{1,0:T(8,128)(2,1)S(1)}, u32[]{:S(2)}, u32[]{:S(2)}) collective-permute-start(bf16[128,1024]{1,0:T(8,128)(2,1)S(1)} %get-tuple-element.111), channel_id=1, source_target_pairs={{0,0},{1,8},{4,4},{5,12},{8,1},{9,9},{12,5},{13,13},{2,2},{3,10},{... | collective-permute-start | bytes 786440 | tf_op jit(solution)/shard_map/ppermute | solution.py:460
  22.4 19.0 %collective-permute-start.9 = (bf16[128,1024]{1,0:T(8,128)(2,1)S(1)}, bf16[128,1024]{1,0:T(8,128)(2,1)S(1)}, u32[]{:S(2)}, u32[]{:S(2)}) collective-permute-start(bf16[128,1024]{1,0:T(8,128)(2,1)S(1)} %get-tuple-element.110), channel_id=1, source_target_pairs={{0,4},{1,12},{4,0},{5,8},{8,5},{9,13},{12,1},{13,9},{2,6},{3,14},{... | collective-permute-start | bytes 786440 | tf_op jit(solution)/shard_map/ppermute | solution.py:460
  23.0 11.4 %collective-permute-start.5 = (bf16[464,256]{1,0:T(8,128)(2,1)S(1)}, bf16[464,256]{1,0:T(8,128)(2,1)S(1)}, u32[]{:S(2)}, u32[]{:S(2)}) collective-permute-start(bf16[464,256]{1,0:T(8,128)(2,1)S(1)} %get-tuple-element.60.refs_1_), channel_id=1, source_target_pairs={{0,16},{16,32},{32,48},{48,64},{64,80},{80,96},{96,112},{112,128},... | collective-permute-start | bytes 712712 | tf_op jit(solution)/shard_map/ppermute | solution.py:40
  24.7 18.7 %collective-permute-start.7 = (bf16[576,256]{1,0:T(8,128)(2,1)S(1)}, bf16[576,256]{1,0:T(8,128)(2,1)S(1)}, u32[]{:S(2)}, u32[]{:S(2)}) collective-permute-start(bf16[576,256]{1,0:T(8,128)(2,1)S(1)} %get-tuple-element.62), channel_id=1, source_target_pairs={{0,1},{1,0},{2,3},{3,2},{4,5},{5,4},{6,7},{7,6},{8,9},{9,8},{10,11... | collective-permute-start | bytes 884744 | tf_op jit(solution)/shard_map/ppermute | solution.py:465
  24.8 9.7 %collective-permute-start.6 = (bf16[320,256]{1,0:T(8,128)(2,1)S(1)}, bf16[320,256]{1,0:T(8,128)(2,1)S(1)}, u32[]{:S(2)}, u32[]{:S(2)}) collective-permute-start(bf16[320,256]{1,0:T(8,128)(2,1)S(1)} %get-tuple-element.61), channel_id=1, source_target_pairs={{0,240},{16,0},{32,16},{48,32},{64,48},{80,64},{96,80},{112,96},{1... | collective-permute-start | bytes 491528 | tf_op jit(solution)/shard_map/ppermute | solution.py:40
  34.5 22.3 %collective-permute-start.13 = (bf16[720,256]{1,0:T(8,128)(2,1)S(1)}, bf16[720,256]{1,0:T(8,128)(2,1)S(1)}, u32[]{:S(2)}, u32[]{:S(2)}) collective-permute-start(bf16[720,256]{1,0:T(8,128)(2,1)S(1)} %get-tuple-element.73), channel_id=1, source_target_pairs={{0,1},{1,0},{2,3},{3,2},{4,5},{5,4},{6,7},{7,6},{8,9},{9,8},{10,11... | collective-permute-start | bytes 1105928 | tf_op jit(solution)/shard_map/ppermute | solution.py:465
  35.9 9.7 %collective-permute-start.11 = (bf16[320,256]{1,0:T(8,128)(2,1)S(1)}, bf16[320,256]{1,0:T(8,128)(2,1)S(1)}, u32[]{:S(2)}, u32[]{:S(2)}) collective-permute-start(bf16[320,256]{1,0:T(8,128)(2,1)S(1)} %collective-permute-done.6.seven_ref.refs_1_.refs_3_), channel_id=1, source_target_pairs={{0,240},{16,0},{32,16},{48,32},{64,48},{80,64},{96,80},{112,96},{1... | collective-permute-start | bytes 491528 | tf_op jit(solution)/shard_map/ppermute | solution.py:40
  41.4 9.0 %collective-permute-start.10 = (bf16[320,256]{1,0:T(8,128)(2,1)S(1)}, bf16[320,256]{1,0:T(8,128)(2,1)S(1)}, u32[]{:S(2)}, u32[]{:S(2)}) collective-permute-start(bf16[320,256]{1,0:T(8,128)(2,1)S(1)} %get-tuple-element.63), channel_id=1, source_target_pairs={{0,16},{16,32},{32,48},{48,64},{64,80},{80,96},{96,112},{112,128},... | collective-permute-start | bytes 491528 | tf_op jit(solution)/shard_map/ppermute | solution.py:40
  50.4 6.6 %collective-permute-start.12 = (bf16[576,256]{1,0:T(8,128)(2,1)S(1)}, bf16[576,256]{1,0:T(8,128)(2,1)S(1)}, u32[]{:S(2)}, u32[]{:S(2)}) collective-permute-start(bf16[576,256]{1,0:T(8,128)(2,1)S(1)} %shard_map.87), channel_id=1, source_target_pairs={{0,1},{1,0},{2,3},{3,2},{4,5},{5,4},{6,7},{7,6},{8,9},{9,8},{10,11... | collective-permute-start | bytes 884744 | tf_op jit(solution)/shard_map/ppermute | solution.py:465
  51.7 9.3 %collective-permute-start.14 = (bf16[320,256]{1,0:T(8,128)(2,1)S(1)}, bf16[320,256]{1,0:T(8,128)(2,1)S(1)}, u32[]{:S(2)}, u32[]{:S(2)}) collective-permute-start(bf16[320,256]{1,0:T(8,128)(2,1)S(1)} %collective-permute-done.10.first_ref.refs_0_.refs_4_), channel_id=1, source_target_pairs={{0,16},{16,32},{32,48},{48,64},{64,80},{80,96},{96,112},{112,128},... | collective-permute-start | bytes 491528 | tf_op jit(solution)/shard_map/ppermute | solution.py:40
  51.7 9.3 %collective-permute-start.15 = (bf16[320,256]{1,0:T(8,128)(2,1)S(1)}, bf16[320,256]{1,0:T(8,128)(2,1)S(1)}, u32[]{:S(2)}, u32[]{:S(2)}) collective-permute-start(bf16[320,256]{1,0:T(8,128)(2,1)S(1)} %collective-permute-done.11.second_ref.refs_1_.refs_5_), channel_id=1, source_target_pairs={{0,240},{16,0},{32,16},{48,32},{64,48},{80,64},{96,80},{112,96},{1... | collective-permute-start | bytes 491528 | tf_op jit(solution)/shard_map/ppermute | solution.py:40
  61.0 13.0 %collective-permute-start.18 = (bf16[576,256]{1,0:T(8,128)(2,1)S(1)}, bf16[576,256]{1,0:T(8,128)(2,1)S(1)}, u32[]{:S(2)}, u32[]{:S(2)}) collective-permute-start(bf16[576,256]{1,0:T(8,128)(2,1)S(1)} %shard_map.89), channel_id=1, source_target_pairs={{0,1},{1,0},{2,3},{3,2},{4,5},{5,4},{6,7},{7,6},{8,9},{9,8},{10,11... | collective-permute-start | bytes 884744 | tf_op jit(solution)/shard_map/ppermute | solution.py:465
  62.0 9.3 %collective-permute-start.16 = (bf16[320,256]{1,0:T(8,128)(2,1)S(1)}, bf16[320,256]{1,0:T(8,128)(2,1)S(1)}, u32[]{:S(2)}, u32[]{:S(2)}) collective-permute-start(bf16[320,256]{1,0:T(8,128)(2,1)S(1)} %collective-permute-done.14.refs_0_.refs_6_.first_ref), channel_id=1, source_target_pairs={{0,16},{16,32},{32,48},{48,64},{64,80},{80,96},{96,112},{112,128},... | collective-permute-start | bytes 491528 | tf_op jit(solution)/shard_map/ppermute | solution.py:40
  71.4 5.1 %collective-permute-start.17 = (bf16[320,256]{1,0:T(8,128)(2,1)S(1)}, bf16[320,256]{1,0:T(8,128)(2,1)S(1)}, u32[]{:S(2)}, u32[]{:S(2)}) collective-permute-start(bf16[320,256]{1,0:T(8,128)(2,1)S(1)} %get-tuple-element.94.refs_1_), channel_id=1, source_target_pairs={{0,1},{1,0},{2,3},{3,2},{4,5},{5,4},{6,7},{7,6},{8,9},{9,8},{10,11... | collective-permute-start | bytes 491528 | tf_op jit(solution)/shard_map/ppermute | solution.py:465
  72.4 4.1 %collective-permute-start.19 = (f32[32,128]{1,0:T(8,128)S(1)}, f32[32,128]{1,0:T(8,128)S(1)}, u32[]{:S(2)}, u32[]{:S(2)}) collective-permute-start(f32[32,128]{1,0:T(8,128)S(1)} %get-tuple-element.105), channel_id=1, source_target_pairs={{0,8},{4,12},{8,0},{12,4},{1,9},{5,13},{9,1},{13,5},{2,10},{6,14},... | collective-permute-start | bytes 49160 | tf_op jit(solution)/shard_map/ppermute | solution.py:533
  76.9 11.8 %collective-permute-start.20 = (bf16[144,1024]{1,0:T(8,128)(2,1)S(1)}, bf16[144,1024]{1,0:T(8,128)(2,1)S(1)}, u32[]{:S(2)}, u32[]{:S(2)}) collective-permute-start(bf16[144,1024]{1,0:T(8,128)(2,1)S(1)} %attend_last.2), channel_id=1, source_target_pairs={{0,0},{8,1},{4,4},{12,5},{1,8},{9,9},{5,12},{13,13},{2,2},{10,3},{... | collective-permute-start | bytes 884744 | tf_op jit(solution)/shard_map/ppermute | solution.py:551
  82.0 9.1 %collective-permute-start.21 = (bf16[144,1024]{1,0:T(8,128)(2,1)S(1)}, bf16[144,1024]{1,0:T(8,128)(2,1)S(1)}, u32[]{:S(2)}, u32[]{:S(2)}) collective-permute-start(bf16[144,1024]{1,0:T(8,128)(2,1)S(1)} %attend_last.3), channel_id=1, source_target_pairs={{4,0},{12,1},{0,4},{8,5},{5,8},{13,9},{1,12},{9,13},{6,2},{14,3},{... | collective-permute-start | bytes 884744 | tf_op jit(solution)/shard_map/ppermute | solution.py:551

commit v3 on v2

--- a/solution.py
+++ b/solution.py
@@ -178,12 +178,11 @@
     put(out_ref, HALF, got(first_ref, BLOCK) + got(second_ref, BLOCK) + energy)
 
 
-def once_kernel(own_ref, eight_ref, up_ref, down_ref, both_ref):
-    both = got(own_ref, HALF) + got(eight_ref, HALF)
-    up_ref[0:HALF, :] = own_ref[0:HALF, :]
+def once_kernel(own_ref, eight_ref, one_ref, up_ref, down_ref, three_ref):
+    up_ref[0:HALF, :] = one_ref[0:HALF, :]
     down_ref[0:HALF, :] = eight_ref[0:HALF, :]
-    put(up_ref, HALF, both)
-    put(down_ref, HALF, both)
+    put(up_ref, HALF, got(one_ref, HALF) + got(eight_ref, HALF))
+    put(down_ref, HALF, got(own_ref, HALF) + got(eight_ref, HALF))
     for odd in range(2):
 
         @pl.when(place()[2] == odd)
@@ -191,15 +190,15 @@
             row = (1 - odd) * BLOCK
             up_ref[HALF + RIDER : HALF + RIDER + BLOCK, :] = eight_ref[row : row + BLOCK, :]
 
-    both_ref[0:HALF, :] = own_ref[0:HALF, :]
-    both_ref[HALF : 2 * HALF, :] = eight_ref[0:HALF, :]
-
-
-def split_kernel(one_ref, seven_ref, next_ref, both_ref):
-    next_ref[...] = one_ref[0 : HALF + RIDER, :]
-    both_ref[0:HALF, :] = one_ref[0:HALF, :]
+    for n, ref in enumerate((own_ref, eight_ref, one_ref)):
+        three_ref[n * HALF : (n + 1) * HALF, :] = ref[0:HALF, :]
+
+
+def split_kernel(two_ref, seven_ref, next_ref, both_ref):
+    next_ref[...] = two_ref[0 : HALF + RIDER, :]
+    both_ref[0:HALF, :] = two_ref[0:HALF, :]
     both_ref[HALF : 2 * HALF, :] = seven_ref[0:HALF, :]
-    both_ref[2 * HALF : 2 * HALF + BLOCK, :] = one_ref[HALF + RIDER : HALF + RIDER + BLOCK, :]
+    both_ref[2 * HALF : 2 * HALF + BLOCK, :] = two_ref[HALF + RIDER : HALF + RIDER + BLOCK, :]
 
 
 def pair_kernel(first_ref, second_ref, both_ref):
@@ -207,10 +206,14 @@
     both_ref[HALF : 2 * HALF, :] = second_ref[0:HALF, :]
 
 
-def total_kernel(*refs):
-    *terms, out_ref, energy_ref = refs
-    out_ref[0:HALF, :] = terms[0][0:HALF, :]
-    total = functools.reduce(jnp.add, [got(ref, HALF) for ref in terms])
+def total_kernel(four_ref, five_ref, own_ref, eight_ref, one_ref, *refs):
+    two_ref, three_ref, seven_ref, six_ref, twelve_ref, out_ref, energy_ref = refs
+    out_ref[0:HALF, :] = four_ref[0:HALF, :]
+    out_ref[HALF + RIDER : 2 * HALF + RIDER, :] = five_ref[0:HALF, :]
+    total = got(own_ref, HALF) + got(eight_ref, HALF) + got(one_ref, HALF)
+    total += got(two_ref, HALF) + got(three_ref, HALF) + got(four_ref, HALF)
+    total += got(seven_ref, HALF) + got(six_ref, HALF) + got(five_ref, HALF)
+    total += got(twelve_ref, 0)
     put(out_ref, HALF, total)
     lane = lax.broadcasted_iota(jnp.int32, (RIDER, 128), 1) // 64
     row = lax.broadcasted_iota(jnp.int32, (RIDER, 128), 0)
@@ -457,7 +460,9 @@
     for t, array in enumerate((send0, send1)):
         kv.append(lax.ppermute(array, COLUMN, to_heads(t)))
     slices = [lax.dynamic_slice_in_dim(queries, (odd ^ t) * 1024, 1024, 1) for t in range(2)]
-    q = [lax.ppermute(slices[t], COLUMN, to_heads(t)) for t in range(2)]
+    q = []
+    for t in range(2):
+        q.append(lax.ppermute(slices[t], COLUMN, to_heads(t)))
     energy = added(energy, "c", 1)
     energy = added(energy, "xl", 1)
 
@@ -473,76 +478,66 @@
 
     message = rows(HALF + RIDER)
     (own,) = small(start_kernel, [message], *kv, energy)
-    eight = shifted(own, 8)
+    eight, one = shifted(own, 8), shifted(own, 1)
+    twelve = shifted(own[HALF:], -4)
     up, down, both = small(
-        once_kernel, [rows(HALF + RIDER + BLOCK), message, rows(2 * HALF)], own, eight
-    )
-    one, seven = shifted(up, 1), shifted(down, -1)
-    other_zero_eight = partner(both)
-
-    onward, both = small(split_kernel, [message, rows(2 * HALF + BLOCK)], one, seven)
-    two, six = shifted(onward, 1), shifted(seven, -1)
-    other_one_seven = partner(both)
-    own, onward = lax.optimization_barrier((own, onward))
-    state = attend(q, [own, eight], ((piece(0, 0, 0, False), piece(1, 0, 8, False)),), None)
+        once_kernel, [rows(HALF + RIDER + BLOCK), message, rows(3 * HALF)], own, eight, one
+    )
+    two, seven = shifted(up, 1), shifted(down, -1)
+    other_first = partner(both)
+    near, up = lax.optimization_barrier((own, up))
+    state = attend(q, [near, eight], ((piece(0, 0, 0, False), piece(1, 0, 8, False)),), None)
     state = attend(
         None,
-        [one, seven, other_zero_eight],
+        [one, other_first],
         (
-            (piece(0, 0, 1, False), piece(1, 0, 7, False)),
-            (piece(2, 0, 0, True), piece(2, HALF, 8, True)),
+            (piece(0, 0, 1, False), piece(1, 2 * HALF, 1, True)),
+            (piece(1, 0, 0, True), piece(1, HALF, 8, True)),
         ),
         state,
     )
 
-    two, six = after(state, two, six)
-    three, five = shifted(two, 1), shifted(six, -1)
-    (both,) = small(pair_kernel, [rows(2 * HALF)], two, six)
-    other_two_six = partner(both)
+    two, seven = after(state, two, seven)
+    onward, both = small(split_kernel, [message, rows(2 * HALF + BLOCK)], two, seven)
+    three, six = shifted(onward, 1), shifted(seven, -1)
+    other_two_seven = partner(both)
+    state = attend(None, [two, seven], ((piece(0, 0, 2, False), piece(1, 0, 7, False)),), state)
     state = attend(
-        None,
-        [two, six, other_one_seven],
-        (
-            (piece(0, 0, 2, False), piece(1, 0, 6, False)),
-            (piece(2, 0, 1, True), piece(2, HALF, 7, True)),
-        ),
-        state,
-    )
-    state = attend(None, [other_two_six], ((piece(0, 0, 2, True), piece(0, HALF, 6, True)),), state)
-
-    three, five = after(state, three, five)
-    four = shifted(three, 1)
-    (both,) = small(pair_kernel, [rows(2 * HALF)], three, five)
-    other_three_five = partner(both)
-    state = attend(None, [three, five], ((piece(0, 0, 3, False), piece(1, 0, 5, False)),), state)
-
-    (four,) = after(state, four)
-    four, energy = small(
+        None, [other_two_seven], ((piece(0, 0, 2, True), piece(0, HALF, 7, True)),), state
+    )
+
+    three, six = after(state, three, six)
+    four, five = shifted(three, 1), shifted(six, -1)
+    (both,) = small(pair_kernel, [rows(2 * HALF)], three, six)
+    other_three_six = partner(both)
+    state = attend(None, [three, six], ((piece(0, 0, 3, False), piece(1, 0, 6, False)),), state)
+
+    four, five = after(state, four, five)
+    last, energy = small(
         total_kernel,
-        [message, jax.ShapeDtypeStruct((RIDER, 128), jnp.float32)],
+        [rows(2 * HALF + RIDER), jax.ShapeDtypeStruct((RIDER, 128), jnp.float32)],
         four,
-        up,
+        five,
+        own,
+        eight,
         one,
+        two,
+        three,
         seven,
-        two,
         six,
-        three,
-        five,
-    )
-    other_four = partner(four)
+        twelve,
+    )
+    other_last = partner(last)
     energy = lax.ppermute(energy, "y", [(i, i ^ 2) for i in range(4)])
     state = attend(
-        None, [other_three_five], ((piece(0, 0, 3, True), piece(0, HALF, 5, True)),), state
+        None, [other_three_six], ((piece(0, 0, 3, True), piece(0, HALF, 6, True)),), state
     )
     units = (
-        (
-            piece(1, 0, 4, False),
-            piece(2, HALF + RIDER, 9, False),
-            piece(3, 2 * HALF, 9, True),
-        ),
-        (piece(0, 0, 4, True),),
-    )
-    arrays = [other_four, four, one, other_one_seven]
+        (piece(1, 0, 4, False), piece(1, HALF + RIDER, 5, False)),
+        (piece(2, HALF + RIDER, 9, False), piece(3, 2 * HALF, 9, True)),
+        (piece(0, 0, 4, True), piece(0, HALF + RIDER, 5, True)),
+    )
+    arrays = [other_last, last, two, other_two_seven]
     back = []
     for t in range(2):
         (mixed,) = attend(

time: 93.3 us -> 91.7 us (0.983)
  the two profiles are of different devices: /device:TPU:1 before, /device:TPU:7 now
where the time goes in v3:
time: 91.7 us; the launch traced here: 91.5 us
  starting transfers between devices  42.1 us (46%)
  waiting for transfers between devices  26.2 us (29%)
  Pallas kernels  21.6 us (24%)
    pallas_call x8, Pallas kernels, attend(): pl.pallas_call(functools.partial(attend_kernel, len(arrays), units, tiles...  18.4 us
    ppermute x9, starting transfers between devices, shifted(): lax.ppermute(array, RING, [(i, (i + by) % SLABS) for i in range(SLABS)])  18.2 us
    ppermute x9, waiting for transfers between devices, shifted(): lax.ppermute(array, RING, [(i, (i + by) % SLABS) for i in range(SLABS)])  10 us
    ppermute x4, starting transfers between devices, partner(): return lax.ppermute(array, 'c', [(0, 1), (1, 0)])  8.37 us
    ppermute x2, waiting for transfers between devices, body(): back.append(lax.ppermute(mixed, COLUMN, [(d, s) for s, d in to_heads(t)]))  7.5 us
    ppermute x2, starting transfers between devices, body(): kv.append(lax.ppermute(array, COLUMN, to_heads(t)))  5.98 us
    ppermute x2, starting transfers between devices, body(): back.append(lax.ppermute(mixed, COLUMN, [(d, s) for s, d in to_heads(t)]))  4.58 us
    ppermute x2, starting transfers between devices, body(): q.append(lax.ppermute(slices[t], COLUMN, to_heads(t)))  4.41 us
  transfers between devices with their start and end apart: 22, of which 10 were waited for; matrix products, arithmetic and copies ran while one was open for 1% of the time, Pallas kernels for 18%

profile of v3, /device:TPU:7, one launch (start us, length us, event | category | flops | bytes accessed | tf_op | source)
XLA Modules:
  0.0 91.5 jit_solution(15065036040215273152)
XLA Ops:
  0.6 2.2 %prepare.1 = (bf16[176,256]{1,0:T(8,128)(2,1)}, bf16[176,256]{1,0:T(8,128)(2,1)}, bf16[128,128]{1,0:T(8,128)(2,1)}, f32[8,128]{1,0:T(8,128)}) custom-call(bf16[128,256]{1,0:T(8,128)(2,1)} %keys_hbm.1, bf16[128,256]{1,0:T(8,128)(2,1)} %values_hbm.1, s32[1,128]{1,0:T(1,128)} %bitcast.4, bf16[2,2,32,128]{3,2,1,0:T(8,128)(2,1)} %bitcast.3), custom_call_target="tpu_custom_call" | custom-call | tf_op jit(solution)/shard_map/prepare/pallas_call | solution.py:439
  2.8 5.4 %collective-permute-start = (bf16[176,256]{1,0:T(8,128)(2,1)}, bf16[176,256]{1,0:T(8,128)(2,1)S(1)}, u32[]{:S(2)}, u32[]{:S(2)}) collective-permute-start(bf16[176,256]{1,0:T(8,128)(2,1)} %get-tuple-element.58), channel_id=1, source_target_pairs={{0,0},{1,8},{4,4},{5,12},{8,1},{9,9},{12,5},{13,13},{2,2},{3,10},{... | collective-permute-start | bytes 270344 | tf_op jit(solution)/shard_map/ppermute | solution.py:461
  8.2 0.6 collective-permute-start.1
  8.8 0.0 collective-permute-start.2
  8.8 1.4 %collective-permute-done.2 = f32[8,128]{1,0:T(8,128)S(1)} collective-permute-done((f32[8,128]{1,0:T(8,128)}, f32[8,128]{1,0:T(8,128)S(1)}, u32[]{:S(2)}, u32[]{:S(2)}) %collective-permute-start.2) | collective-permute-done | bytes 4128 | tf_op jit(solution)/shard_map/ppermute | solution.py:45
  10.2 0.7 add.12
  10.9 0.5 collective-permute-start.3
  11.4 1.9 %collective-permute-done.3 = f32[8,128]{1,0:T(8,128)S(1)} collective-permute-done((f32[8,128]{1,0:T(8,128)S(1)}, f32[8,128]{1,0:T(8,128)S(1)}, u32[]{:S(2)}, u32[]{:S(2)}) %collective-permute-start.3) | collective-permute-done | bytes 4128 | tf_op jit(solution)/shard_map/ppermute | solution.py:45
  13.3 0.0 collective-permute-done.first_ref
  13.3 0.3 collective-permute-done.1.second_ref
  13.7 1.7 %collective-permute-start.4 = (bf16[320,256]{1,0:T(8,128)(2,1)S(1)}, bf16[320,256]{1,0:T(8,128)(2,1)S(1)}, u32[]{:S(2)}, u32[]{:S(2)}) collective-permute-start(bf16[320,256]{1,0:T(8,128)(2,1)S(1)} %shard_map.84.own_ref.refs_2_), channel_id=1, source_target_pairs={{0,16},{16,32},{32,48},{48,64},{64,80},{80,96},{96,112},{112,128},... | collective-permute-start | bytes 491528 | tf_op jit(solution)/shard_map/ppermute | solution.py:40
  15.4 1.1 %collective-permute-start.5 = (bf16[320,256]{1,0:T(8,128)(2,1)S(1)}, bf16[320,256]{1,0:T(8,128)(2,1)S(1)}, u32[]{:S(2)}, u32[]{:S(2)}) collective-permute-start(bf16[320,256]{1,0:T(8,128)(2,1)S(1)} %shard_map.84.own_ref.refs_2_), channel_id=1, source_target_pairs={{0,128},{16,144},{32,160},{48,176},{64,192},{80,208},{96,224},{112... | collective-permute-start | bytes 491528 | tf_op jit(solution)/shard_map/ppermute | solution.py:40
  16.5 7.3 %collective-permute-done.4.one_ref.refs_0_ = bf16[320,256]{1,0:T(8,128)(2,1)S(1)} collective-permute-done((bf16[320,256]{1,0:T(8,128)(2,1)S(1)}, bf16[320,256]{1,0:T(8,128)(2,1)S(1)}, u32[]{:S(2)}, u32[]{:S(2)}) %collective-permute-start.4) | collective-permute-done | bytes 163872 | tf_op jit(solution)/shard_map/ppermute | solution.py:40
  23.8 0.0 collective-permute-done.5.eight_ref.refs_3_
  23.8 0.1 shard_map.85
  23.9 3.3 %collective-permute-start.6 = (bf16[864,256]{1,0:T(8,128)(2,1)S(1)}, bf16[864,256]{1,0:T(8,128)(2,1)S(1)}, u32[]{:S(2)}, u32[]{:S(2)}) collective-permute-start(bf16[864,256]{1,0:T(8,128)(2,1)S(1)} %get-tuple-element.61), channel_id=1, source_target_pairs={{0,1},{1,0},{2,3},{3,2},{4,5},{5,4},{6,7},{7,6},{8,9},{9,8},{10,11... | collective-permute-start | bytes 1327112 | tf_op jit(solution)/shard_map/ppermute | solution.py:470
  27.3 3.3 %collective-permute-start.7 = (bf16[128,1024]{1,0:T(8,128)(2,1)S(1)}, bf16[128,1024]{1,0:T(8,128)(2,1)S(1)}, u32[]{:S(2)}, u32[]{:S(2)}) collective-permute-start(bf16[128,1024]{1,0:T(8,128)(2,1)S(1)} %get-tuple-element.113), channel_id=1, source_target_pairs={{0,0},{1,8},{4,4},{5,12},{8,1},{9,9},{12,5},{13,13},{2,2},{3,10},{... | collective-permute-start | bytes 786440 | tf_op jit(solution)/shard_map/ppermute | solution.py:465
  30.6 1.1 %collective-permute-start.8 = (bf16[128,1024]{1,0:T(8,128)(2,1)S(1)}, bf16[128,1024]{1,0:T(8,128)(2,1)S(1)}, u32[]{:S(2)}, u32[]{:S(2)}) collective-permute-start(bf16[128,1024]{1,0:T(8,128)(2,1)S(1)} %get-tuple-element.112), channel_id=1, source_target_pairs={{0,4},{1,12},{4,0},{5,8},{8,5},{9,13},{12,1},{13,9},{2,6},{3,14},{... | collective-permute-start | bytes 786440 | tf_op jit(solution)/shard_map/ppermute | solution.py:465
  31.7 0.0 collective-permute-start.9
  31.7 5.1 %collective-permute-start.10 = (bf16[320,256]{1,0:T(8,128)(2,1)S(1)}, bf16[320,256]{1,0:T(8,128)(2,1)S(1)}, u32[]{:S(2)}, u32[]{:S(2)}) collective-permute-start(bf16[320,256]{1,0:T(8,128)(2,1)S(1)} %get-tuple-element.70), channel_id=1, source_target_pairs={{0,240},{16,0},{32,16},{48,32},{64,48},{80,64},{96,80},{112,96},{1... | collective-permute-start | bytes 491528 | tf_op jit(solution)/shard_map/ppermute | solution.py:40
  36.7 1.1 %collective-permute-done.7.refs_0_ = bf16[128,1024]{1,0:T(8,128)(2,1)S(1)} collective-permute-done((bf16[128,1024]{1,0:T(8,128)(2,1)S(1)}, bf16[128,1024]{1,0:T(8,128)(2,1)S(1)}, u32[]{:S(2)}, u32[]{:S(2)}) %collective-permute-start.7) | collective-permute-done | bytes 262176 | tf_op jit(solution)/shard_map/ppermute | solution.py:465
  37.8 2.0 %collective-permute-done.8.refs_1_ = bf16[128,1024]{1,0:T(8,128)(2,1)S(1)} collective-permute-done((bf16[128,1024]{1,0:T(8,128)(2,1)S(1)}, bf16[128,1024]{1,0:T(8,128)(2,1)S(1)}, u32[]{:S(2)}, u32[]{:S(2)}) %collective-permute-start.8) | collective-permute-done | bytes 262176 | tf_op jit(solution)/shard_map/ppermute | solution.py:465
  39.9 2.1 %attend.6 = (bf16[2048,128]{1,0:T(8,128)(2,1)S(1)}, f32[32,128]{1,0:T(8,128)S(1)}, f32[2048,128]{1,0:T(8,128)S(1)}, f32[2048,128]{1,0:T(8,128)S(1)}, f32[2048,128]{1,0:T(8,128)S(1)}) custom-call(bf16[128,1024]{1,0:T(8,128)(2,1)S(1)} %collective-permute-done.7.refs_0_, bf16[128,1024]{1,0:T(8,128)(2,1)S(1)} %collective-permute-done.8.refs_1_, ...), custom_call_target="tpu_custom_call" | custom-call | flops 536870912 | bytes 1048576 | tf_op jit(solution)/shard_map/attend/pallas_call | solution.py:421
  41.9 3.7 %attend.7 = (bf16[2048,128]{1,0:T(8,128)(2,1)S(1)}, f32[32,128]{1,0:T(8,128)S(1)}, f32[2048,128]{1,0:T(8,128)S(1)}, f32[2048,128]{1,0:T(8,128)S(1)}, f32[2048,128]{1,0:T(8,128)S(1)}) custom-call(bf16[320,256]{1,0:T(8,128)(2,1)S(1)} %collective-permute-done.4.one_ref.refs_0_, ...), custom_call_target="tpu_custom_call", output_to_operand_aliasing={{0}: (2, {}), {1}: (3, {}), {2}: (4, {}), {3}: (5, {}), {4}... | custom-call | flops 1073741824 | bytes 1048576 | tf_op jit(solution)/shard_map/attend/pallas_call | solution.py:421
  45.7 0.0 collective-permute-done.10.seven_ref.refs_1_.refs_2_
  45.7 0.0 collective-permute-done.9.two_ref.refs_0_.refs_2_
  45.7 0.3 collective-permute-start.11
  46.0 0.1 collective-permute-start.12
  46.1 5.1 %collective-permute-start.13 = (bf16[320,256]{1,0:T(8,128)(2,1)S(1)}, bf16[320,256]{1,0:T(8,128)(2,1)S(1)}, u32[]{:S(2)}, u32[]{:S(2)}) collective-permute-start(bf16[320,256]{1,0:T(8,128)(2,1)S(1)} %collective-permute-done.10.seven_ref.refs_1_.refs_2_), channel_id=1, source_target_pairs={{0,240},{16,0},{32,16},{48,32},{64,48},{80,64},{96,80},{112,96},{1... | collective-permute-start | bytes 491528 | tf_op jit(solution)/shard_map/ppermute | solution.py:40
  51.2 1.9 %attend.8 = (bf16[2048,128]{1,0:T(8,128)(2,1)S(1)}, f32[32,128]{1,0:T(8,128)S(1)}, f32[2048,128]{1,0:T(8,128)S(1)}, f32[2048,128]{1,0:T(8,128)S(1)}, f32[2048,128]{1,0:T(8,128)S(1)}) custom-call(bf16[464,256]{1,0:T(8,128)(2,1)S(1)} %collective-permute-done.9.two_ref.refs_0_.refs_2_, ...), custom_call_target="tpu_custom_call", output_to_operand_aliasing={{0}: (2, {}), {1}: (3, {}), {2}: (4, {}), {3}: (5, {}), {4}... | custom-call | flops 536870912 | bytes 1048576 | tf_op jit(solution)/shard_map/attend/pallas_call | solution.py:421
  53.1 0.0 collective-permute-done.11.refs_0_.refs_3_
  53.1 1.9 %attend.9 = (bf16[2048,128]{1,0:T(8,128)(2,1)S(1)}, f32[32,128]{1,0:T(8,128)S(1)}, f32[2048,128]{1,0:T(8,128)S(1)}, f32[2048,128]{1,0:T(8,128)S(1)}, f32[2048,128]{1,0:T(8,128)S(1)}) custom-call(bf16[720,256]{1,0:T(8,128)(2,1)S(1)} %collective-permute-done.11.refs_0_.refs_3_, ...), custom_call_target="tpu_custom_call", output_to_operand_aliasing={{0}: (1, {}), {1}: (2, {}), {2}: (3, {}), {3}: (4, {}), {4}... | custom-call | flops 536870912 | bytes 1048576 | tf_op jit(solution)/shard_map/attend/pallas_call | solution.py:421
  55.1 0.1 collective-permute-start.14
  55.2 5.1 %collective-permute-start.15 = (bf16[320,256]{1,0:T(8,128)(2,1)S(1)}, bf16[320,256]{1,0:T(8,128)(2,1)S(1)}, u32[]{:S(2)}, u32[]{:S(2)}) collective-permute-start(bf16[320,256]{1,0:T(8,128)(2,1)S(1)} %collective-permute-done.13.refs_1_.refs_3_.second_ref), channel_id=1, source_target_pairs={{0,240},{16,0},{32,16},{48,32},{64,48},{80,64},{96,80},{112,96},{1... | collective-permute-start | bytes 491528 | tf_op jit(solution)/shard_map/ppermute | solution.py:40
  60.3 1.8 %collective-permute-start.18 = (bf16[576,256]{1,0:T(8,128)(2,1)S(1)}, bf16[576,256]{1,0:T(8,128)(2,1)S(1)}, u32[]{:S(2)}, u32[]{:S(2)}) collective-permute-start(bf16[576,256]{1,0:T(8,128)(2,1)S(1)} %shard_map.88), channel_id=1, source_target_pairs={{0,1},{1,0},{2,3},{3,2},{4,5},{5,4},{6,7},{7,6},{8,9},{9,8},{10,11... | collective-permute-start | bytes 884744 | tf_op jit(solution)/shard_map/ppermute | solution.py:470
  62.1 1.9 %attend.10 = (bf16[2048,128]{1,0:T(8,128)(2,1)S(1)}, f32[32,128]{1,0:T(8,128)S(1)}, f32[2048,128]{1,0:T(8,128)S(1)}, f32[2048,128]{1,0:T(8,128)S(1)}, f32[2048,128]{1,0:T(8,128)S(1)}) custom-call(bf16[320,256]{1,0:T(8,128)(2,1)S(1)} %collective-permute-done.12.refs_0_.refs_1_.first_ref, ...), custom_call_target="tpu_custom_call", output_to_operand_aliasing={{0}: (2, {}), {1}: (3, {}), {2}: (4, {}), {3}: (5, {}), {4}... | custom-call | flops 536870912 | bytes 1048576 | tf_op jit(solution)/shard_map/attend/pallas_call | solution.py:421
  64.0 2.7 %collective-permute-done.16.refs_4_ = bf16[32,256]{1,0:T(8,128)(2,1)S(1)} collective-permute-done((bf16[32,256]{1,0:T(8,128)(2,1)S(1)}, bf16[32,256]{1,0:T(8,128)(2,1)S(1)}, u32[]{:S(2)}, u32[]{:S(2)}) %collective-permute-start.16) | collective-permute-done | bytes 16416 | tf_op jit(solution)/shard_map/ppermute | solution.py:40
  66.7 0.1 shard_map.87
  66.8 3.0 %collective-permute-start.17 = (bf16[608,256]{1,0:T(8,128)(2,1)S(1)}, bf16[608,256]{1,0:T(8,128)(2,1)S(1)}, u32[]{:S(2)}, u32[]{:S(2)}) collective-permute-start(bf16[608,256]{1,0:T(8,128)(2,1)S(1)} %get-tuple-element.96.refs_1_), channel_id=1, source_target_pairs={{0,1},{1,0},{2,3},{3,2},{4,5},{5,4},{6,7},{7,6},{8,9},{9,8},{10,11... | collective-permute-start | bytes 933896 | tf_op jit(solution)/shard_map/ppermute | solution.py:470
  69.8 2.1 %attend.11 = (bf16[2048,128]{1,0:T(8,128)(2,1)S(1)}, f32[32,128]{1,0:T(8,128)S(1)}, f32[2048,128]{1,0:T(8,128)S(1)}, f32[2048,128]{1,0:T(8,128)S(1)}, f32[2048,128]{1,0:T(8,128)S(1)}) custom-call(bf16[576,256]{1,0:T(8,128)(2,1)S(1)} %collective-permute-done.18.refs_0_, ...), custom_call_target="tpu_custom_call", output_to_operand_aliasing={{0}: (1, {}), {1}: (2, {}), {2}: (3, {}), {3}: (4, {}), {4}... | custom-call | flops 536870912 | bytes 1048576 | tf_op jit(solution)/shard_map/attend/pallas_call | solution.py:421
  71.9 1.9 %collective-permute-done.19.refs_9_ = f32[32,128]{1,0:T(8,128)S(1)} collective-permute-done((f32[32,128]{1,0:T(8,128)S(1)}, f32[32,128]{1,0:T(8,128)S(1)}, u32[]{:S(2)}, u32[]{:S(2)}) %collective-permute-start.19) | collective-permute-done | bytes 16416 | tf_op jit(solution)/shard_map/ppermute | solution.py:531
  73.8 2.4 %attend_last.2 = bf16[144,1024]{1,0:T(8,128)(2,1)S(1)} custom-call(bf16[608,256]{1,0:T(8,128)(2,1)S(1)} %collective-permute-done.17.refs_0_, bf16[608,256]{1,0:T(8,128)(2,1)S(1)} %get-tuple-element.96.refs_1_, bf16[464,256]{1,0:T(8,128)(2,1)S(1)} %collective-permute-done.9.two_ref.refs_0_.refs_2_, ...), custom_call_target="tpu_custom_call" | custom-call | flops 671088640 | bytes 1048576 | tf_op jit(solution)/shard_map/attend_last/pallas_call | solution.py:421
  76.2 3.2 %collective-permute-start.20 = (bf16[144,1024]{1,0:T(8,128)(2,1)S(1)}, bf16[144,1024]{1,0:T(8,128)(2,1)S(1)}, u32[]{:S(2)}, u32[]{:S(2)}) collective-permute-start(bf16[144,1024]{1,0:T(8,128)(2,1)S(1)} %attend_last.2), channel_id=1, source_target_pairs={{0,0},{8,1},{4,4},{12,5},{1,8},{9,9},{5,12},{13,13},{2,2},{10,3},{... | collective-permute-start | bytes 884744 | tf_op jit(solution)/shard_map/ppermute | solution.py:546
  79.4 2.4 %attend_last.3 = bf16[144,1024]{1,0:T(8,128)(2,1)S(1)} custom-call(bf16[608,256]{1,0:T(8,128)(2,1)S(1)} %collective-permute-done.17.refs_0_, bf16[608,256]{1,0:T(8,128)(2,1)S(1)} %get-tuple-element.96.refs_1_, bf16[464,256]{1,0:T(8,128)(2,1)S(1)} %collective-permute-done.9.two_ref.refs_0_.refs_2_, ...), custom_call_target="tpu_custom_call" | custom-call | flops 671088640 | bytes 1048576 | tf_op jit(solution)/shard_map/attend_last/pallas_call | solution.py:421
  81.8 1.4 %collective-permute-start.21 = (bf16[144,1024]{1,0:T(8,128)(2,1)S(1)}, bf16[144,1024]{1,0:T(8,128)(2,1)S(1)}, u32[]{:S(2)}, u32[]{:S(2)}) collective-permute-start(bf16[144,1024]{1,0:T(8,128)(2,1)S(1)} %attend_last.3), channel_id=1, source_target_pairs={{4,0},{12,1},{0,4},{8,5},{5,8},{13,9},{1,12},{9,13},{6,2},{14,3},{... | collective-permute-start | bytes 884744 | tf_op jit(solution)/shard_map/ppermute | solution.py:546
  83.2 5.1 %collective-permute-done.20.first_ref = bf16[144,1024]{1,0:T(8,128)(2,1)S(1)} collective-permute-done((bf16[144,1024]{1,0:T(8,128)(2,1)S(1)}, bf16[144,1024]{1,0:T(8,128)(2,1)S(1)}, u32[]{:S(2)}, u32[]{:S(2)}) %collective-permute-start.20) | collective-permute-done | bytes 294944 | tf_op jit(solution)/shard_map/ppermute | solution.py:546
  88.3 2.4 %collective-permute-done.21.second_ref = bf16[144,1024]{1,0:T(8,128)(2,1)S(1)} collective-permute-done((bf16[144,1024]{1,0:T(8,128)(2,1)S(1)}, bf16[144,1024]{1,0:T(8,128)(2,1)S(1)}, u32[]{:S(2)}, u32[]{:S(2)}) %collective-permute-start.21) | collective-permute-done | bytes 294944 | tf_op jit(solution)/shard_map/ppermute | solution.py:546
  90.7 0.8 shard_map.89
  (17 shorter events, 0.1 us)
Async XLA Ops:
  0.6 26.6 %copy-start = (bf16[128,2048]{1,0:T(8,128)(2,1)S(1)}, bf16[128,2048]{1,0:T(8,128)(2,1)}, u32[]{:S(2)}) copy-start(bf16[128,2048]{1,0:T(8,128)(2,1)} %param.5) | copy-start | bytes 1572868
  2.8 10.5 %collective-permute-start = (bf16[176,256]{1,0:T(8,128)(2,1)}, bf16[176,256]{1,0:T(8,128)(2,1)S(1)}, u32[]{:S(2)}, u32[]{:S(2)}) collective-permute-start(bf16[176,256]{1,0:T(8,128)(2,1)} %get-tuple-element.58), channel_id=1, source_target_pairs={{0,0},{1,8},{4,4},{5,12},{8,1},{9,9},{12,5},{13,13},{2,2},{3,10},{... | collective-permute-start | bytes 270344 | tf_op jit(solution)/shard_map/ppermute | solution.py:461
  8.2 5.5 %collective-permute-start.1 = (bf16[176,256]{1,0:T(8,128)(2,1)}, bf16[176,256]{1,0:T(8,128)(2,1)S(1)}, u32[]{:S(2)}, u32[]{:S(2)}) collective-permute-start(bf16[176,256]{1,0:T(8,128)(2,1)} %get-tuple-element.59), channel_id=1, source_target_pairs={{0,4},{1,12},{4,0},{5,8},{8,5},{9,13},{12,1},{13,9},{2,6},{3,14},{... | collective-permute-start | bytes 270344 | tf_op jit(solution)/shard_map/ppermute | solution.py:461
  8.8 1.4 %collective-permute-start.2 = (f32[8,128]{1,0:T(8,128)}, f32[8,128]{1,0:T(8,128)S(1)}, u32[]{:S(2)}, u32[]{:S(2)}) collective-permute-start(f32[8,128]{1,0:T(8,128)} %get-tuple-element.60), channel_id=1, source_target_pairs={{0,1},{1,0},{2,3},{3,2},{4,5},{5,4},{6,7},{7,6},{8,9},{9,8},{10,11... | collective-permute-start | bytes 12296 | tf_op jit(solution)/shard_map/ppermute | solution.py:45
  10.9 2.5 %collective-permute-start.3 = (f32[8,128]{1,0:T(8,128)S(1)}, f32[8,128]{1,0:T(8,128)S(1)}, u32[]{:S(2)}, u32[]{:S(2)}) collective-permute-start(f32[8,128]{1,0:T(8,128)S(1)} %add.12), channel_id=1, source_target_pairs={{0,2},{2,0},{1,3},{3,1},{4,6},{6,4},{5,7},{7,5},{8,10},{10,8},{9,1... | collective-permute-start | bytes 12296 | tf_op jit(solution)/shard_map/ppermute | solution.py:45
  13.7 10.1 %collective-permute-start.4 = (bf16[320,256]{1,0:T(8,128)(2,1)S(1)}, bf16[320,256]{1,0:T(8,128)(2,1)S(1)}, u32[]{:S(2)}, u32[]{:S(2)}) collective-permute-start(bf16[320,256]{1,0:T(8,128)(2,1)S(1)} %shard_map.84.own_ref.refs_2_), channel_id=1, source_target_pairs={{0,16},{16,32},{32,48},{48,64},{64,80},{80,96},{96,112},{112,128},... | collective-permute-start | bytes 491528 | tf_op jit(solution)/shard_map/ppermute | solution.py:40
  15.4 8.4 %collective-permute-start.5 = (bf16[320,256]{1,0:T(8,128)(2,1)S(1)}, bf16[320,256]{1,0:T(8,128)(2,1)S(1)}, u32[]{:S(2)}, u32[]{:S(2)}) collective-permute-start(bf16[320,256]{1,0:T(8,128)(2,1)S(1)} %shard_map.84.own_ref.refs_2_), channel_id=1, source_target_pairs={{0,128},{16,144},{32,160},{48,176},{64,192},{80,208},{96,224},{112... | collective-permute-start | bytes 491528 | tf_op jit(solution)/shard_map/ppermute | solution.py:40
  23.9 18.0 %collective-permute-start.6 = (bf16[864,256]{1,0:T(8,128)(2,1)S(1)}, bf16[864,256]{1,0:T(8,128)(2,1)S(1)}, u32[]{:S(2)}, u32[]{:S(2)}) collective-permute-start(bf16[864,256]{1,0:T(8,128)(2,1)S(1)} %get-tuple-element.61), channel_id=1, source_target_pairs={{0,1},{1,0},{2,3},{3,2},{4,5},{5,4},{6,7},{7,6},{8,9},{9,8},{10,11... | collective-permute-start | bytes 1327112 | tf_op jit(solution)/shard_map/ppermute | solution.py:470
  27.3 10.6 %collective-permute-start.7 = (bf16[128,1024]{1,0:T(8,128)(2,1)S(1)}, bf16[128,1024]{1,0:T(8,128)(2,1)S(1)}, u32[]{:S(2)}, u32[]{:S(2)}) collective-permute-start(bf16[128,1024]{1,0:T(8,128)(2,1)S(1)} %get-tuple-element.113), channel_id=1, source_target_pairs={{0,0},{1,8},{4,4},{5,12},{8,1},{9,9},{12,5},{13,13},{2,2},{3,10},{... | collective-permute-start | bytes 786440 | tf_op jit(solution)/shard_map/ppermute | solution.py:465
  30.6 9.3 %collective-permute-start.8 = (bf16[128,1024]{1,0:T(8,128)(2,1)S(1)}, bf16[128,1024]{1,0:T(8,128)(2,1)S(1)}, u32[]{:S(2)}, u32[]{:S(2)}) collective-permute-start(bf16[128,1024]{1,0:T(8,128)(2,1)S(1)} %get-tuple-element.112), channel_id=1, source_target_pairs={{0,4},{1,12},{4,0},{5,8},{8,5},{9,13},{12,1},{13,9},{2,6},{3,14},{... | collective-permute-start | bytes 786440 | tf_op jit(solution)/shard_map/ppermute | solution.py:465
  31.7 14.0 %collective-permute-start.9 = (bf16[464,256]{1,0:T(8,128)(2,1)S(1)}, bf16[464,256]{1,0:T(8,128)(2,1)S(1)}, u32[]{:S(2)}, u32[]{:S(2)}) collective-permute-start(bf16[464,256]{1,0:T(8,128)(2,1)S(1)} %get-tuple-element.62), channel_id=1, source_target_pairs={{0,16},{16,32},{32,48},{48,64},{64,80},{80,96},{96,112},{112,128},... | collective-permute-start | bytes 712712 | tf_op jit(solution)/shard_map/ppermute | solution.py:40
  31.7 14.0 %collective-permute-start.10 = (bf16[320,256]{1,0:T(8,128)(2,1)S(1)}, bf16[320,256]{1,0:T(8,128)(2,1)S(1)}, u32[]{:S(2)}, u32[]{:S(2)}) collective-permute-start(bf16[320,256]{1,0:T(8,128)(2,1)S(1)} %get-tuple-element.70), channel_id=1, source_target_pairs={{0,240},{16,0},{32,16},{48,32},{64,48},{80,64},{96,80},{112,96},{1... | collective-permute-start | bytes 491528 | tf_op jit(solution)/shard_map/ppermute | solution.py:40
  45.7 7.4 %collective-permute-start.11 = (bf16[720,256]{1,0:T(8,128)(2,1)S(1)}, bf16[720,256]{1,0:T(8,128)(2,1)S(1)}, u32[]{:S(2)}, u32[]{:S(2)}) collective-permute-start(bf16[720,256]{1,0:T(8,128)(2,1)S(1)} %get-tuple-element.73), channel_id=1, source_target_pairs={{0,1},{1,0},{2,3},{3,2},{4,5},{5,4},{6,7},{7,6},{8,9},{9,8},{10,11... | collective-permute-start | bytes 1105928 | tf_op jit(solution)/shard_map/ppermute | solution.py:470
  46.0 9.0 %collective-permute-start.12 = (bf16[320,256]{1,0:T(8,128)(2,1)S(1)}, bf16[320,256]{1,0:T(8,128)(2,1)S(1)}, u32[]{:S(2)}, u32[]{:S(2)}) collective-permute-start(bf16[320,256]{1,0:T(8,128)(2,1)S(1)} %get-tuple-element.85), channel_id=1, source_target_pairs={{0,16},{16,32},{32,48},{48,64},{64,80},{80,96},{96,112},{112,128},... | collective-permute-start | bytes 491528 | tf_op jit(solution)/shard_map/ppermute | solution.py:40
  46.1 9.0 %collective-permute-start.13 = (bf16[320,256]{1,0:T(8,128)(2,1)S(1)}, bf16[320,256]{1,0:T(8,128)(2,1)S(1)}, u32[]{:S(2)}, u32[]{:S(2)}) collective-permute-start(bf16[320,256]{1,0:T(8,128)(2,1)S(1)} %collective-permute-done.10.seven_ref.refs_1_.refs_2_), channel_id=1, source_target_pairs={{0,240},{16,0},{32,16},{48,32},{64,48},{80,64},{96,80},{112,96},{1... | collective-permute-start | bytes 491528 | tf_op jit(solution)/shard_map/ppermute | solution.py:40
  55.1 8.9 %collective-permute-start.14 = (bf16[320,256]{1,0:T(8,128)(2,1)S(1)}, bf16[320,256]{1,0:T(8,128)(2,1)S(1)}, u32[]{:S(2)}, u32[]{:S(2)}) collective-permute-start(bf16[320,256]{1,0:T(8,128)(2,1)S(1)} %collective-permute-done.12.refs_0_.refs_1_.first_ref), channel_id=1, source_target_pairs={{0,16},{16,32},{32,48},{48,64},{64,80},{80,96},{96,112},{112,128},... | collective-permute-start | bytes 491528 | tf_op jit(solution)/shard_map/ppermute | solution.py:40
  55.2 8.8 %collective-permute-start.15 = (bf16[320,256]{1,0:T(8,128)(2,1)S(1)}, bf16[320,256]{1,0:T(8,128)(2,1)S(1)}, u32[]{:S(2)}, u32[]{:S(2)}) collective-permute-start(bf16[320,256]{1,0:T(8,128)(2,1)S(1)} %collective-permute-done.13.refs_1_.refs_3_.second_ref), channel_id=1, source_target_pairs={{0,240},{16,0},{32,16},{48,32},{64,48},{80,64},{96,80},{112,96},{1... | collective-permute-start | bytes 491528 | tf_op jit(solution)/shard_map/ppermute | solution.py:40
  60.2 6.5 %collective-permute-start.16 = (bf16[32,256]{1,0:T(8,128)(2,1)S(1)}, bf16[32,256]{1,0:T(8,128)(2,1)S(1)}, u32[]{:S(2)}, u32[]{:S(2)}) collective-permute-start(bf16[32,256]{1,0:T(8,128)(2,1)S(1)} %slice.4), channel_id=1, source_target_pairs={{0,192},{16,208},{32,224},{48,240},{64,0},{80,16},{96,32},{112,48}... | collective-permute-start | bytes 49160 | tf_op jit(solution)/shard_map/ppermute | solution.py:40
  60.3 9.5 %collective-permute-start.18 = (bf16[576,256]{1,0:T(8,128)(2,1)S(1)}, bf16[576,256]{1,0:T(8,128)(2,1)S(1)}, u32[]{:S(2)}, u32[]{:S(2)}) collective-permute-start(bf16[576,256]{1,0:T(8,128)(2,1)S(1)} %shard_map.88), channel_id=1, source_target_pairs={{0,1},{1,0},{2,3},{3,2},{4,5},{5,4},{6,7},{7,6},{8,9},{9,8},{10,11... | collective-permute-start | bytes 884744 | tf_op jit(solution)/shard_map/ppermute | solution.py:470
  66.8 7.1 %collective-permute-start.17 = (bf16[608,256]{1,0:T(8,128)(2,1)S(1)}, bf16[608,256]{1,0:T(8,128)(2,1)S(1)}, u32[]{:S(2)}, u32[]{:S(2)}) collective-permute-start(bf16[608,256]{1,0:T(8,128)(2,1)S(1)} %get-tuple-element.96.refs_1_), channel_id=1, source_target_pairs={{0,1},{1,0},{2,3},{3,2},{4,5},{5,4},{6,7},{7,6},{8,9},{9,8},{10,11... | collective-permute-start | bytes 933896 | tf_op jit(solution)/shard_map/ppermute | solution.py:470
  69.7 4.1 %collective-permute-start.19 = (f32[32,128]{1,0:T(8,128)S(1)}, f32[32,128]{1,0:T(8,128)S(1)}, u32[]{:S(2)}, u32[]{:S(2)}) collective-permute-start(f32[32,128]{1,0:T(8,128)S(1)} %get-tuple-element.107), channel_id=1, source_target_pairs={{0,8},{4,12},{8,0},{12,4},{1,9},{5,13},{9,1},{13,5},{2,10},{6,14},... | collective-permute-start | bytes 49160 | tf_op jit(solution)/shard_map/ppermute | solution.py:531
  76.2 12.1 %collective-permute-start.20 = (bf16[144,1024]{1,0:T(8,128)(2,1)S(1)}, bf16[144,1024]{1,0:T(8,128)(2,1)S(1)}, u32[]{:S(2)}, u32[]{:S(2)}) collective-permute-start(bf16[144,1024]{1,0:T(8,128)(2,1)S(1)} %attend_last.2), channel_id=1, source_target_pairs={{0,0},{8,1},{4,4},{12,5},{1,8},{9,9},{5,12},{13,13},{2,2},{10,3},{... | collective-permute-start | bytes 884744 | tf_op jit(solution)/shard_map/ppermute | solution.py:546
  81.8 8.9 %collective-permute-start.21 = (bf16[144,1024]{1,0:T(8,128)(2,1)S(1)}, bf16[144,1024]{1,0:T(8,128)(2,1)S(1)}, u32[]{:S(2)}, u32[]{:S(2)}) collective-permute-start(bf16[144,1024]{1,0:T(8,128)(2,1)S(1)} %attend_last.3), channel_id=1, source_target_pairs={{4,0},{12,1},{0,4},{8,5},{5,8},{13,9},{1,12},{9,13},{6,2},{14,3},{... | collective-permute-start | bytes 884744 | tf_op jit(solution)/shard_map/ppermute | solution.py:546
